TPU v7x, 512 devices: a whole 4x4x16 slice. The times are simulated.
512 devices in a mesh: gz: 16 (over z_lo, core), gy: 8 (over y, z_hi), gx: 4 (over x).
Axes of the slice: x: 4, y: 4, z: 16 (z_hi: 2, z_lo: 8; z = z_hi * 8 + z_lo), core: 2. Of those that a mesh axis runs over, the one named last changes fastest.
Arguments:
- velocity: float32 [3, 128, 128, 2048], P(None, 'gx', 'gy', 'gz'), may hold values from -3.5 to 5.5
- pressure: float32 [128, 128, 2048], P('gx', 'gy', 'gz'), may hold values from -6 to 6
- voidage: float32 [128, 128, 2048], P('gx', 'gy', 'gz'), may hold values from 0.5 to 0.95
- particle_vel: float32 [3, 128, 128, 2048], P(None, 'gx', 'gy', 'gz'), may hold values from -6 to 6
- forcing: float32 [1], replicated, may hold values from 0.5 to 2
- target_flux: float32 [1], replicated, may hold values from 0.5 to 1.5
Outputs:
- vel_new: float32 [3, 128, 128, 2048], P(None, 'gx', 'gy', 'gz')
- source: float32 [128, 128, 2048], P('gx', 'gy', 'gz')
- forcing_new: float32 [1], replicated
All inputs are finite; a program needn't handle non-finite values.
Results may differ from a plain program's by a relative error of at most 0.000079.
Values sent between devices are 32-bit elements; how exact they have to be, the bound alone decides.
A program may use at most 64 MiB of HBM per device.

v0:
```python
import jax
import jax.numpy as jnp
from jax import lax
from jax.sharding import Mesh
from jax.sharding import PartitionSpec as P

GY = ("gy_0", "gy_1")
GZ = ("gz_0", "gz_1")
GZ_GY_GX = ("gz_0", "gz_1", "gy_0", "gy_1", "gx")


time_step = 0.2
viscosity = 0.1
drag_scale = 1.0


def with_halo(value, sides, width):
    edges = {}
    for axis, dim in sides:
        count, length = (lax.axis_size(axis), value.shape[dim])
        up = [(i, (i + 1) % count) for i in range(count)]
        last = lax.slice_in_dim(value, length - width, length, axis=dim)
        leading = lax.slice_in_dim(value, 0, width, axis=dim)
        edges[dim] = (
            lax.ppermute(last, axis, up),
            lax.ppermute(leading, axis, [(b, a) for a, b in up]),
        )
    done = []
    for _, dim in sides:
        low, high = edges[dim]
        around = [(width, width) if d in done else (0, 0) for d in range(value.ndim)]
        value = jnp.concatenate([jnp.pad(low, around), value, jnp.pad(high, around)], axis=dim)
        done.append(dim)
    return value


def over_axes(value, axes):
    for axis in axes:
        value = lax.psum(value, axis)
    return value


def shifted(field, axis_no, offset):
    slices = [slice(1, -1)] * 3
    length = field.shape[field.ndim - 3 + axis_no]
    slices[axis_no] = slice(1 + offset, length - 1 + offset)
    return field[tuple([slice(None)] * (field.ndim - 3) + slices)]


def upward():
    return (jnp.arange(3) == 2).astype(jnp.float32).reshape(3, 1, 1, 1)


def predict(vel_pad, pres_pad, voidage, particle_vel, forcing):
    centre = shifted(vel_pad, 0, 0)
    advection = jnp.zeros_like(centre)
    laplace = -6.0 * centre
    grads = []
    for axis_no in range(3):
        upper = shifted(vel_pad, axis_no, 1)
        lower = shifted(vel_pad, axis_no, -1)
        advection = advection + centre[axis_no] * (upper - lower) * 0.5
        laplace = laplace + upper + lower
        grads.append((shifted(pres_pad, axis_no, 1) - shifted(pres_pad, axis_no, -1)) * 0.5)
    forces = -advection + viscosity * laplace - jnp.stack(grads) + forcing * upward()
    slip_speed = jnp.sqrt(jnp.sum((centre - particle_vel) ** 2, axis=0))
    drag_rate = drag_scale * (1.0 - voidage) * voidage ** (-2.65) * (1.0 + slip_speed)
    return (centre + time_step * (forces + drag_rate * particle_vel)) / (
        1.0 + time_step * drag_rate
    )


def edge_fill(field, axis_no, depth, at_low, at_high):
    length = field.shape[axis_no]
    low_part = lax.slice_in_dim(field, 0, depth, axis=axis_no)
    inner = lax.slice_in_dim(field, depth, length - depth, axis=axis_no)
    high_part = lax.slice_in_dim(field, length - depth, length, axis=axis_no)
    first = lax.slice_in_dim(field, depth, depth + 1, axis=axis_no)
    last = lax.slice_in_dim(field, length - depth - 1, length - depth, axis=axis_no)
    low_part = jnp.where(at_low, first, low_part)
    high_part = jnp.where(at_high, last, high_part)
    return jnp.concatenate([low_part, inner, high_part], axis=axis_no)


def outside(length, depth, at_low, at_high):
    positions = jnp.arange(length)
    return at_low & (positions < depth) | at_high & (positions >= length - depth)


def wall_zero(field, depth, x_low, x_high, y_low, y_high):
    walls = (
        outside(field.shape[-3], depth, x_low, x_high)[:, None]
        | outside(field.shape[-2], depth, y_low, y_high)[None, :]
    )
    return jnp.where(walls[:, :, None], 0.0, field)


def local(velocity, pressure, voidage, particle_vel, forcing, target_flux):
    x_index = lax.axis_index("gx")
    x_low = x_index == 0
    x_high = x_index == lax.axis_size("gx") - 1
    y_index = lax.axis_index(GY)
    y_low = y_index == 0
    y_high = y_index == lax.axis_size(GY) - 1
    cells = voidage.size * lax.axis_size("gx") * lax.axis_size(GY) * lax.axis_size(GZ)
    stacked = jnp.concatenate([velocity, pressure[None]], axis=0)
    padded = with_halo(stacked, ((GZ, 3), (GY, 2), ("gx", 1)), 1)
    vel_pad = wall_zero(padded[:3], 1, x_low, x_high, y_low, y_high)
    pres_pad = edge_fill(edge_fill(padded[3], 0, 1, x_low, x_high), 1, 1, y_low, y_high)
    ustar = predict(vel_pad, pres_pad, voidage, particle_vel, forcing[0])
    flux_stack = jnp.concatenate([voidage * ustar, voidage[None]], axis=0)
    flux_joined = with_halo(flux_stack, ((GZ, 3), (GY, 2), ("gx", 1)), 1)
    flux_pad = wall_zero(flux_joined, 1, x_low, x_high, y_low, y_high)
    divergence = jnp.zeros_like(voidage)
    for axis_no in range(3):
        divergence = (
            divergence
            + (shifted(flux_pad[axis_no], axis_no, 1) - shifted(flux_pad[axis_no], axis_no, -1))
            * 0.5
        )
    void_slope = (shifted(flux_pad[3], 2, 1) - shifted(flux_pad[3], 2, -1)) * 0.5
    flow_part = jnp.sum(voidage * ustar[2])
    flow_sum, void_sum = (over_axes(flow_part, GZ_GY_GX), over_axes(jnp.sum(voidage), GZ_GY_GX))
    force_step = (target_flux[0] * cells - flow_sum) / (time_step * void_sum)
    vel_new = ustar + time_step * force_step * upward()
    source = divergence + time_step * force_step * void_slope
    return (vel_new, source, forcing + force_step)


def solution(mesh):
    finer = Mesh(
        mesh.devices.reshape(8, 2, 4, 2, mesh.shape["gx"]), ("gz_0", "gz_1", "gy_0", "gy_1", "gx")
    )
    placed = (
        P(None, "gx", GY, GZ),
        P("gx", GY, GZ),
        P("gx", GY, GZ),
        P(None, "gx", GY, GZ),
        P(),
        P(),
    )
    return jax.shard_map(
        local,
        mesh=finer,
        in_specs=placed,
        out_specs=(P(None, "gx", GY, GZ), P("gx", GY, GZ), P()),
        check_vma=False,
    )
```

profile of v0, /device:TPU:32, one launch (start us, length us, event | category | flops | bytes accessed | tf_op | source)
XLA Modules:
  0.0 167.5 jit_solution(3244609470606286661)
XLA Ops:
  0.6 2.0 %fusion.15 = (f32[4,32,16,1]{3,2,1,0:T(8,128)S(1)}, f32[4,32,16,1]{3,2,1,0:T(8,128)S(1)}) fusion(f32[3,32,16,128]{3,2,1,0:T(8,128)} %param.6, f32[1,32,16,128]{3,2,1,0:T(8,128)} %bitcast.40), kind=kLoop, calls=%fused_computation.38 | loop fusion | flops 4096 | bytes 1064960 | tf_op jit(solution)/shard_map/concatenate | solution.py:106
  3.1 1.9 %collective-permute-start.2 = (f32[4,32,16,1]{1,2,3,0:T(8,128)S(1)}, f32[4,32,16,1]{1,2,3,0:T(8,128)S(1)}, u32[]{:S(2)}, u32[]{:S(2)}) collective-permute-start(f32[4,32,16,1]{1,2,3,0:T(8,128)S(1)} %copy.137), channel_id=1, source_target_pairs={{0,32},{32,64},{64,96},{96,128},{128,160},{160,192},{192,224},{224... | collective-permute-start | bytes 24584 | tf_op jit(solution)/shard_map/ppermute | solution.py:25
  5.6 3.6 %collective-permute-start.3 = (f32[4,32,16,1]{1,2,3,0:T(8,128)S(1)}, f32[4,32,16,1]{1,2,3,0:T(8,128)S(1)}, u32[]{:S(2)}, u32[]{:S(2)}) collective-permute-start(f32[4,32,16,1]{1,2,3,0:T(8,128)S(1)} %copy.138), channel_id=1, source_target_pairs={{32,0},{64,32},{96,64},{128,96},{160,128},{192,160},{224,192},{256... | collective-permute-start | bytes 24584 | tf_op jit(solution)/shard_map/ppermute | solution.py:26
  9.3 14.8 %collective-permute-start.1 = (f32[4,32,1,128]{3,2,1,0:T(1,128)S(1)}, f32[4,32,1,128]{3,2,1,0:T(1,128)S(1)}, u32[]{:S(2)}, u32[]{:S(2)}) collective-permute-start(f32[4,32,1,128]{3,2,1,0:T(1,128)S(1)} %get-tuple-element.45), channel_id=1, source_target_pairs={{0,4},{4,8},{8,12},{12,16},{16,20},{20,24},{24,28},{28,0},{1,5},{5... | collective-permute-start | bytes 196616 | tf_op jit(solution)/shard_map/ppermute | solution.py:25
  24.2 4.4 %collective-permute-start.4 = (f32[4,32,1,128]{3,2,1,0:T(1,128)S(1)}, f32[4,32,1,128]{3,2,1,0:T(1,128)S(1)}, u32[]{:S(2)}, u32[]{:S(2)}) collective-permute-start(f32[4,32,1,128]{3,2,1,0:T(1,128)S(1)} %get-tuple-element.46), channel_id=1, source_target_pairs={{4,0},{8,4},{12,8},{16,12},{20,16},{24,20},{28,24},{0,28},{5,1},{9... | collective-permute-start | bytes 196616 | tf_op jit(solution)/shard_map/ppermute | solution.py:26
  28.5 0.6 pad_maximum_fusion.10
  29.2 3.4 %collective-permute-start = (f32[4,1,16,128]{3,2,1,0:T(8,128)}, f32[4,1,16,128]{3,2,1,0:T(8,128)S(1)}, u32[]{:S(2)}, u32[]{:S(2)}) collective-permute-start(f32[4,1,16,128]{3,2,1,0:T(8,128)} %get-tuple-element.47), channel_id=1, source_target_pairs={{0,1},{1,2},{2,3},{3,0},{4,5},{5,6},{6,7},{7,4},{8,9},{9,10},{10,1... | collective-permute-start | bytes 98312 | tf_op jit(solution)/shard_map/ppermute | solution.py:25
  33.3 3.7 %collective-permute-start.5 = (f32[4,1,16,128]{3,2,1,0:T(8,128)S(1)}, f32[4,1,16,128]{3,2,1,0:T(8,128)S(1)}, u32[]{:S(2)}, u32[]{:S(2)}) collective-permute-start(f32[4,1,16,128]{3,2,1,0:T(8,128)S(1)} %get-tuple-element.48), channel_id=1, source_target_pairs={{1,0},{2,1},{3,2},{0,3},{5,4},{6,5},{7,6},{4,7},{9,8},{10,9},{11,1... | collective-permute-start | bytes 98312 | tf_op jit(solution)/shard_map/ppermute | solution.py:26
  37.7 0.5 copy.123
  38.2 0.5 copy.124
  39.6 0.6 collective-permute-done.4
  41.5 2.3 %fusion.12 = f32[3,34,18,130]{3,2,1,0:T(8,128)S(1)} fusion(f32[3,32,16,128]{3,2,1,0:T(8,128)S(1)} %copy-done, f32[1,32,16,128]{3,2,1,0:T(8,128)S(1)} %bitcast.45, f32[4,1,18,130]{3,2,1,0:T(8,128)S(1)} %pad.29, f32[4,1,18,130]{3,2,1,0:T(8,128)S(1)} %pad.26, f32[4,32,1,130]{3,2,1,0:T(1,128)S(1)} %pad.28, f32[4,32,1,130]{3,2,1,0:T(1,128)S(1)} %pad.27, ...), kind=kLoop, calls=%fused_computation.23 | loop fusion | flops 1909440 | bytes 2228292 | tf_op jit(solution)/shard_map/jit(_where)/select_n | solution.py:95
  45.4 1.3 broadcast_multiply_fusion
  46.7 1.3 fusion.13
  48.2 1.7 %copy.132 = f32[4,32,16,1]{1,2,3,0:T(8,128)S(1)} copy(f32[4,32,16,1]{3,2,1,0:T(8,128)} %get-tuple-element.37) | data formatting | bytes 16384 | tf_op jit(solution)/shard_map/slice | solution.py:22
  49.9 1.9 %collective-permute-start.8 = (f32[4,32,16,1]{1,2,3,0:T(8,128)S(1)}, f32[4,32,16,1]{1,2,3,0:T(8,128)S(1)}, u32[]{:S(2)}, u32[]{:S(2)}) collective-permute-start(f32[4,32,16,1]{1,2,3,0:T(8,128)S(1)} %copy.132), channel_id=1, source_target_pairs={{0,32},{32,64},{64,96},{96,128},{128,160},{160,192},{192,224},{224... | collective-permute-start | bytes 24584 | tf_op jit(solution)/shard_map/ppermute | solution.py:25
  52.3 3.6 %collective-permute-start.9 = (f32[4,32,16,1]{1,2,3,0:T(8,128)S(1)}, f32[4,32,16,1]{1,2,3,0:T(8,128)}, u32[]{:S(2)}, u32[]{:S(2)}) collective-permute-start(f32[4,32,16,1]{1,2,3,0:T(8,128)S(1)} %copy.133), channel_id=1, source_target_pairs={{32,0},{64,32},{96,64},{128,96},{160,128},{192,160},{224,192},{256... | collective-permute-start | bytes 24584 | tf_op jit(solution)/shard_map/ppermute | solution.py:26
  55.9 12.0 %collective-permute-start.10 = (f32[4,32,1,128]{3,2,1,0:T(1,128)S(1)}, f32[4,32,1,128]{3,2,1,0:T(1,128)S(1)}, u32[]{:S(2)}, u32[]{:S(2)}) collective-permute-start(f32[4,32,1,128]{3,2,1,0:T(1,128)S(1)} %get-tuple-element.42), channel_id=1, source_target_pairs={{4,0},{8,4},{12,8},{16,12},{20,16},{24,20},{28,24},{0,28},{5,1},{9... | collective-permute-start | bytes 196616 | tf_op jit(solution)/shard_map/ppermute | solution.py:26
  68.0 2.5 %collective-permute-start.7 = (f32[4,32,1,128]{3,2,1,0:T(1,128)S(1)}, f32[4,32,1,128]{3,2,1,0:T(1,128)S(1)}, u32[]{:S(2)}, u32[]{:S(2)}) collective-permute-start(f32[4,32,1,128]{3,2,1,0:T(1,128)S(1)} %get-tuple-element.41), channel_id=1, source_target_pairs={{0,4},{4,8},{8,12},{12,16},{16,20},{20,24},{24,28},{28,0},{1,5},{5... | collective-permute-start | bytes 196616 | tf_op jit(solution)/shard_map/ppermute | solution.py:25
  70.5 4.7 %collective-permute-start.11 = (f32[4,1,16,128]{3,2,1,0:T(8,128)S(1)}, f32[4,1,16,128]{3,2,1,0:T(8,128)S(1)}, u32[]{:S(2)}, u32[]{:S(2)}) collective-permute-start(f32[4,1,16,128]{3,2,1,0:T(8,128)S(1)} %get-tuple-element.40), channel_id=1, source_target_pairs={{1,0},{2,1},{3,2},{0,3},{5,4},{6,5},{7,6},{4,7},{9,8},{10,9},{11,1... | collective-permute-start | bytes 98312 | tf_op jit(solution)/shard_map/ppermute | solution.py:26
  75.2 0.7 fusion.40
  75.9 41.3 %all-reduce.8 = (f32[]{:T(128)}, f32[]{:T(128)}) all-reduce(f32[]{:T(128)} %get-tuple-element.13, f32[]{:T(128)} %get-tuple-element.12), channel_id=1, replica_groups=mesh['gz_0'=8,'gz_1'=2,'gy_0'=4,'gy_1'=2,'gx'=4] {'gz_0'}, use_global_device_ids=true, to_apply=%region_2.3 | all-reduce | flops 2 | bytes 16 | tf_op jit(solution)/shard_map/psum | solution.py:39
  117.2 3.1 %all-reduce.12 = (f32[]{:T(128)}, f32[]{:T(128)}) all-reduce(f32[]{:T(128)} %get-tuple-element.14, f32[]{:T(128)} %get-tuple-element.15), channel_id=1, replica_groups=mesh['gz_0'=8,'gz_1'=2,'gy_0'=4,'gy_1'=2,'gx'=4] {'gz_1'}, use_global_device_ids=true, to_apply=%region_3.4 | all-reduce | flops 2 | bytes 16 | tf_op jit(solution)/shard_map/psum | solution.py:39
  120.3 8.7 %all-reduce.10 = (f32[]{:T(128)}, f32[]{:T(128)}) all-reduce(f32[]{:T(128)} %get-tuple-element.22, f32[]{:T(128)} %get-tuple-element.23), channel_id=1, replica_groups=mesh['gz_0'=8,'gz_1'=2,'gy_0'=4,'gy_1'=2,'gx'=4] {'gy_0'}, use_global_device_ids=true, to_apply=%region_4.5 | all-reduce | flops 2 | bytes 16 | tf_op jit(solution)/shard_map/psum | solution.py:39
  128.9 14.7 %all-reduce.11 = (f32[]{:T(128)}, f32[]{:T(128)}) all-reduce(f32[]{:T(128)} %get-tuple-element.18, f32[]{:T(128)} %get-tuple-element.19), channel_id=1, replica_groups=mesh['gz_0'=8,'gz_1'=2,'gy_0'=4,'gy_1'=2,'gx'=4] {'gy_1'}, use_global_device_ids=true, to_apply=%region_5.6 | all-reduce | flops 2 | bytes 16 | tf_op jit(solution)/shard_map/psum | solution.py:39
  143.6 8.8 %all-reduce.9 = (f32[]{:T(128)}, f32[]{:T(128)}) all-reduce(f32[]{:T(128)} %get-tuple-element.20, f32[]{:T(128)} %get-tuple-element.21), channel_id=1, replica_groups=mesh['gz_0'=8,'gz_1'=2,'gy_0'=4,'gy_1'=2,'gx'=4] {'gx'}, use_global_device_ids=true, to_apply=%region_6.7 | all-reduce | flops 2 | bytes 16 | tf_op jit(solution)/shard_map/psum | solution.py:39
  153.7 3.7 %collective-permute-start.6 = (f32[4,1,16,128]{3,2,1,0:T(8,128)S(1)}, f32[4,1,16,128]{3,2,1,0:T(8,128)S(1)}, u32[]{:S(2)}, u32[]{:S(2)}) collective-permute-start(f32[4,1,16,128]{3,2,1,0:T(8,128)S(1)} %get-tuple-element.39), channel_id=1, source_target_pairs={{0,1},{1,2},{2,3},{3,0},{4,5},{5,6},{6,7},{7,4},{8,9},{9,10},{10,1... | collective-permute-start | bytes 98312 | tf_op jit(solution)/shard_map/ppermute | solution.py:25
  157.4 1.0 broadcast_add_fusion
  158.4 0.5 copy.134
  159.0 1.3 copy.135
  160.8 4.2 %fusion = f32[4,34,18,130]{3,2,1,0:T(8,128)S(1)} fusion(f32[4,1,16,128]{3,2,1,0:T(8,128)S(1)} %collective-permute-done.11, f32[4,32,1,128]{3,2,1,0:T(1,128)S(1)} %collective-permute-done.10, f32[4,32,1,128]{3,2,1,0:T(1,128)S(1)} %collective-permute-done.7, f32[4,1,16,128]{3,2,1,0:T(8,128)S(1)} %collective-permute-done.6, f32[4,32,16,1]{3,2,1,0:T(8,128)S(1)} %copy.135, ...), kind=kLoop, calls=%fused_computation.3 | loop fusion | flops 7319520 | bytes 2535140 | tf_op jit(solution)/shard_map/jit(_where)/select_n | solution.py:95
  165.2 1.2 fusion.23
  (48 shorter events, 6.1 us)
Async XLA Ops:
  0.6 8.6 %copy-start.2 = (f32[32,16,128]{2,1,0:T(8,128)S(1)}, f32[32,16,128]{2,1,0:T(8,128)}, u32[]{:S(2)}) copy-start(f32[32,16,128]{2,1,0:T(8,128)} %param.7) | copy-start | bytes 786436
  0.6 8.6 %copy-start = (f32[3,32,16,128]{3,2,1,0:T(8,128)S(1)}, f32[3,32,16,128]{3,2,1,0:T(8,128)}, u32[]{:S(2)}) copy-start(f32[3,32,16,128]{3,2,1,0:T(8,128)} %param.6) | copy-start | bytes 2359300
  3.1 30.2 %collective-permute-start.2 = (f32[4,32,16,1]{1,2,3,0:T(8,128)S(1)}, f32[4,32,16,1]{1,2,3,0:T(8,128)S(1)}, u32[]{:S(2)}, u32[]{:S(2)}) collective-permute-start(f32[4,32,16,1]{1,2,3,0:T(8,128)S(1)} %copy.137), channel_id=1, source_target_pairs={{0,32},{32,64},{64,96},{96,128},{128,160},{160,192},{192,224},{224... | collective-permute-start | bytes 24584 | tf_op jit(solution)/shard_map/ppermute | solution.py:25
  5.6 32.6 %collective-permute-start.3 = (f32[4,32,16,1]{1,2,3,0:T(8,128)S(1)}, f32[4,32,16,1]{1,2,3,0:T(8,128)S(1)}, u32[]{:S(2)}, u32[]{:S(2)}) collective-permute-start(f32[4,32,16,1]{1,2,3,0:T(8,128)S(1)} %copy.138), channel_id=1, source_target_pairs={{32,0},{64,32},{96,64},{128,96},{160,128},{192,160},{224,192},{256... | collective-permute-start | bytes 24584 | tf_op jit(solution)/shard_map/ppermute | solution.py:26
  9.3 29.9 %collective-permute-start.1 = (f32[4,32,1,128]{3,2,1,0:T(1,128)S(1)}, f32[4,32,1,128]{3,2,1,0:T(1,128)S(1)}, u32[]{:S(2)}, u32[]{:S(2)}) collective-permute-start(f32[4,32,1,128]{3,2,1,0:T(1,128)S(1)} %get-tuple-element.45), channel_id=1, source_target_pairs={{0,4},{4,8},{8,12},{12,16},{16,20},{20,24},{24,28},{28,0},{1,5},{5... | collective-permute-start | bytes 196616 | tf_op jit(solution)/shard_map/ppermute | solution.py:25
  24.2 16.1 %collective-permute-start.4 = (f32[4,32,1,128]{3,2,1,0:T(1,128)S(1)}, f32[4,32,1,128]{3,2,1,0:T(1,128)S(1)}, u32[]{:S(2)}, u32[]{:S(2)}) collective-permute-start(f32[4,32,1,128]{3,2,1,0:T(1,128)S(1)} %get-tuple-element.46), channel_id=1, source_target_pairs={{4,0},{8,4},{12,8},{16,12},{20,16},{24,20},{28,24},{0,28},{5,1},{9... | collective-permute-start | bytes 196616 | tf_op jit(solution)/shard_map/ppermute | solution.py:26
  29.2 9.6 %collective-permute-start = (f32[4,1,16,128]{3,2,1,0:T(8,128)}, f32[4,1,16,128]{3,2,1,0:T(8,128)S(1)}, u32[]{:S(2)}, u32[]{:S(2)}) collective-permute-start(f32[4,1,16,128]{3,2,1,0:T(8,128)} %get-tuple-element.47), channel_id=1, source_target_pairs={{0,1},{1,2},{2,3},{3,0},{4,5},{5,6},{6,7},{7,4},{8,9},{9,10},{10,1... | collective-permute-start | bytes 98312 | tf_op jit(solution)/shard_map/ppermute | solution.py:25
  33.3 5.8 %collective-permute-start.5 = (f32[4,1,16,128]{3,2,1,0:T(8,128)S(1)}, f32[4,1,16,128]{3,2,1,0:T(8,128)S(1)}, u32[]{:S(2)}, u32[]{:S(2)}) collective-permute-start(f32[4,1,16,128]{3,2,1,0:T(8,128)S(1)} %get-tuple-element.48), channel_id=1, source_target_pairs={{1,0},{2,1},{3,2},{0,3},{5,4},{6,5},{7,6},{4,7},{9,8},{10,9},{11,1... | collective-permute-start | bytes 98312 | tf_op jit(solution)/shard_map/ppermute | solution.py:26
  41.5 2.6 %copy-start.3 = (f32[3,32,16,128]{3,2,1,0:T(8,128)S(1)}, f32[3,32,16,128]{3,2,1,0:T(8,128)}, u32[]{:S(2)}) copy-start(f32[3,32,16,128]{3,2,1,0:T(8,128)} %param.9) | copy-start | bytes 2359300
  41.5 2.9 %copy-start.1 = (f32[32,16,128]{2,1,0:T(8,128)S(1)}, f32[32,16,128]{2,1,0:T(8,128)}, u32[]{:S(2)}) copy-start(f32[32,16,128]{2,1,0:T(8,128)} %param.8) | copy-start | bytes 786436
  49.9 103.8 %collective-permute-start.8 = (f32[4,32,16,1]{1,2,3,0:T(8,128)S(1)}, f32[4,32,16,1]{1,2,3,0:T(8,128)S(1)}, u32[]{:S(2)}, u32[]{:S(2)}) collective-permute-start(f32[4,32,16,1]{1,2,3,0:T(8,128)S(1)} %copy.132), channel_id=1, source_target_pairs={{0,32},{32,64},{64,96},{96,128},{128,160},{160,192},{192,224},{224... | collective-permute-start | bytes 24584 | tf_op jit(solution)/shard_map/ppermute | solution.py:25
  52.3 106.7 %collective-permute-start.9 = (f32[4,32,16,1]{1,2,3,0:T(8,128)S(1)}, f32[4,32,16,1]{1,2,3,0:T(8,128)}, u32[]{:S(2)}, u32[]{:S(2)}) collective-permute-start(f32[4,32,16,1]{1,2,3,0:T(8,128)S(1)} %copy.133), channel_id=1, source_target_pairs={{32,0},{64,32},{96,64},{128,96},{160,128},{192,160},{224,192},{256... | collective-permute-start | bytes 24584 | tf_op jit(solution)/shard_map/ppermute | solution.py:26
  55.9 104.8 %collective-permute-start.10 = (f32[4,32,1,128]{3,2,1,0:T(1,128)S(1)}, f32[4,32,1,128]{3,2,1,0:T(1,128)S(1)}, u32[]{:S(2)}, u32[]{:S(2)}) collective-permute-start(f32[4,32,1,128]{3,2,1,0:T(1,128)S(1)} %get-tuple-element.42), channel_id=1, source_target_pairs={{4,0},{8,4},{12,8},{16,12},{20,16},{24,20},{28,24},{0,28},{5,1},{9... | collective-permute-start | bytes 196616 | tf_op jit(solution)/shard_map/ppermute | solution.py:26
  68.0 92.8 %collective-permute-start.7 = (f32[4,32,1,128]{3,2,1,0:T(1,128)S(1)}, f32[4,32,1,128]{3,2,1,0:T(1,128)S(1)}, u32[]{:S(2)}, u32[]{:S(2)}) collective-permute-start(f32[4,32,1,128]{3,2,1,0:T(1,128)S(1)} %get-tuple-element.41), channel_id=1, source_target_pairs={{0,4},{4,8},{8,12},{12,16},{16,20},{20,24},{24,28},{28,0},{1,5},{5... | collective-permute-start | bytes 196616 | tf_op jit(solution)/shard_map/ppermute | solution.py:25
  70.5 89.8 %collective-permute-start.11 = (f32[4,1,16,128]{3,2,1,0:T(8,128)S(1)}, f32[4,1,16,128]{3,2,1,0:T(8,128)S(1)}, u32[]{:S(2)}, u32[]{:S(2)}) collective-permute-start(f32[4,1,16,128]{3,2,1,0:T(8,128)S(1)} %get-tuple-element.40), channel_id=1, source_target_pairs={{1,0},{2,1},{3,2},{0,3},{5,4},{6,5},{7,6},{4,7},{9,8},{10,9},{11,1... | collective-permute-start | bytes 98312 | tf_op jit(solution)/shard_map/ppermute | solution.py:26
  153.7 7.0 %collective-permute-start.6 = (f32[4,1,16,128]{3,2,1,0:T(8,128)S(1)}, f32[4,1,16,128]{3,2,1,0:T(8,128)S(1)}, u32[]{:S(2)}, u32[]{:S(2)}) collective-permute-start(f32[4,1,16,128]{3,2,1,0:T(8,128)S(1)} %get-tuple-element.39), channel_id=1, source_target_pairs={{0,1},{1,2},{2,3},{3,0},{4,5},{5,6},{6,7},{7,4},{8,9},{9,10},{10,1... | collective-permute-start | bytes 98312 | tf_op jit(solution)/shard_map/ppermute | solution.py:25
where the time goes:
time: 168 us
  blocking collectives  76.5 us (46%)
  starting transfers between devices  60.2 us (36%)
  other arithmetic  16.9 us (10%)
  local copies, waits for them, and re-layouts  7.71 us (5%)
  between operations  4.86 us (3%)
    psum x5, blocking collectives, over_axes(): value = lax.psum(value, axis)  76.5 us
    ppermute x6, starting transfers between devices, with_halo(): lax.ppermute(leading, axis, [(b, a) for a, b in up])  32 us
    ppermute x6, starting transfers between devices, with_halo(): lax.ppermute(last, axis, up)  28.3 us
    select_n x2, other arithmetic, wall_zero(): return jnp.where(walls[:, :, None], 0.0, field)  6.54 us
  transfers between devices with their start and end apart: 12, of which 3 were waited for; matrix products, arithmetic and copies ran while one was open for 4% of the time, Pallas kernels for 0%

commit v1 on v0

v1 whole, which is shorter than its diff:
```python
import jax
import jax.numpy as jnp
from jax import lax
from jax.experimental import pallas as pl
from jax.experimental.pallas import tpu as pltpu
from jax.sharding import PartitionSpec as P

MESH = pl.DeviceIdType.MESH
DT = 0.2
NU = 0.1
BX, BY, BZ = 32, 16, 128
ROWS = BX * BY
PAD = ROWS + 2 * BY
VX, VY, VZ, PR = 0, 1, 2, 3
FVZ, FVY, FP, FVX, FD, FC = 0, 1, 2, 3, 4, 5


def kernel(
    force_ref, target_ref, vel_h, pres_h, eps_h, pv_h,
    vel_o, src_o, force_o,
    V, E, PV, G, S, SL, FX, Q,
    xrecv, zsend, zrecv, zsend2, zrecv2, ysend, yrecv, xsend2,
    row1, red1, row2, red2,
    lsem, xs, xr, zs, zr, zs2, zr2, ys, yr, xs2, xr2, s1, r1, s2, r2,
):
    gz, gy, gx = lax.axis_index("gz"), lax.axis_index("gy"), lax.axis_index("gx")
    ngz, ngy, ngx = 16, 8, 4
    here = {"gz": gz, "gy": gy, "gx": gx}

    def at(**kw):
        return {**here, **kw}

    y, zhi = gy // 2, gy % 2
    zlo, core = gz // 2, gz % 2
    zabs = zhi * 8 + zlo
    xi, yi = gx, y
    has_xlo, has_xhi = gx > 0, gx < ngx - 1
    has_ylo, has_yhi = gy > 0, gy < ngy - 1

    def of_z(z):
        return at(gz=lax.rem(z, 8) * 2 + core, gy=y * 2 + z // 8)

    def of_plane(i):
        return at(gx=i // 8, gy=lax.rem(i // 2, 4) * 2 + zhi, gz=zlo * 2 + lax.rem(i, 2))

    plane = gx * 8 + y * 2 + core
    zpeers = [of_z(lax.rem(zabs + k, 16)) for k in range(1, 16)]
    ppeers = [of_plane(lax.rem(plane + k, 32)) for k in range(1, 32)]
    zlow, zhigh = at(gz=lax.rem(gz + ngz - 1, ngz)), at(gz=lax.rem(gz + 1, ngz))
    ylow, yhigh = at(gy=lax.rem(gy + ngy - 1, ngy)), at(gy=lax.rem(gy + 1, ngy))
    xlow, xhigh = at(gx=lax.rem(gx + ngx - 1, ngx)), at(gx=lax.rem(gx + 1, ngx))

    barrier = pltpu.get_barrier_semaphore()
    partners = [ylow, yhigh] + zpeers + [zlow, zhigh] + ppeers
    for d in partners:
        pl.semaphore_signal(barrier, inc=1, device_id=d, device_id_type=MESH)

    loads = [
        pltpu.make_async_copy(vel_h, V.at[pl.ds(0, 3), pl.ds(BY, ROWS), :], lsem.at[0]),
        pltpu.make_async_copy(pres_h, V.at[3, pl.ds(BY, ROWS), :], lsem.at[1]),
        pltpu.make_async_copy(eps_h, E, lsem.at[2]),
        pltpu.make_async_copy(pv_h, PV, lsem.at[3]),
    ]
    for cp in loads:
        cp.start()

    lane = lax.broadcasted_iota(jnp.int32, (BY, BZ), 1)
    rown = lax.broadcasted_iota(jnp.int32, (BY, BZ), 0)
    zero = jnp.zeros((BY, BZ), jnp.float32)
    for f in range(4):
        V[f, pl.ds(0, BY), :] = zero
        V[f, pl.ds(ROWS + BY, BY), :] = zero
    Q[...] = jnp.zeros_like(Q)
    force = force_ref[0]
    for cp in loads:
        cp.wait()

    def face(side):
        return 0 if side == 0 else BY - 1

    for side in range(2):
        for slot, f in ((FVZ, VZ), (FVY, VY), (FP, PR), (FVX, VX)):
            ysend[side, slot] = V[f, pl.ds(BY + face(side), BX, stride=BY), :]

    def slab(x, carry):
        o = pl.multiple_of(x * BY, BY)
        c = [V[f, pl.ds(o + BY, BY), :] for f in range(4)]
        xm = [V[f, pl.ds(o, BY), :] for f in range(4)]
        xp = [V[f, pl.ds(o + 2 * BY, BY), :] for f in range(4)]
        e = E[pl.ds(o, BY), :]
        pv = [PV[k, pl.ds(o, BY), :] for k in range(3)]
        zm = [jnp.where(lane == 0, 0.0, pltpu.roll(a, 1, 1)) for a in c]
        zp = [jnp.where(lane == BZ - 1, 0.0, pltpu.roll(a, BZ - 1, 1)) for a in c]
        ym = [jnp.where(rown == 0, 0.0, pltpu.roll(a, 1, 0)) for a in c]
        yp = [jnp.where(rown == BY - 1, 0.0, pltpu.roll(a, BY - 1, 0)) for a in c]
        slip = jnp.sqrt(
            (c[0] - pv[0]) * (c[0] - pv[0])
            + (c[1] - pv[1]) * (c[1] - pv[1])
            + (c[2] - pv[2]) * (c[2] - pv[2])
        )
        drag = (1.0 - e) * jnp.exp(-2.65 * jnp.log(e)) * (1.0 + slip)
        w = 1.0 / (1.0 + DT * drag)
        hi, lo = (xp, yp, zp), (xm, ym, zm)
        for k in range(3):
            adv = zero
            lap = -6.0 * c[k]
            for d in range(3):
                adv = adv + c[d] * (hi[d][k] - lo[d][k])
                lap = lap + hi[d][k] + lo[d][k]
            fk = NU * lap - 0.5 * (adv + (hi[k][3] - lo[k][3]))
            if k == 2:
                fk = fk + force
            vel_o[k, pl.ds(o, BY), :] = (c[k] + DT * (fk + drag * pv[k])) * w
        G[pl.ds(o, BY), :] = DT * w
        s = zero
        for k, a in enumerate(c + [e]):
            s = jnp.where(lane == k, a if k == 0 else pltpu.roll(a, k, 1), s)
            s = jnp.where(lane == 8 + k, pltpu.roll(a, 9 + k, 1), s)
        S[pl.ds(o, BY), :] = s
        return carry

    lax.fori_loop(0, BX, slab, 0)

    def pack(dst):
        for i in range(4):
            t = S[pl.ds(BZ * i, BZ), :].T
            dst[0, :, pl.ds(BZ * i, BZ)] = t[0:8]
            dst[1, :, pl.ds(BZ * i, BZ)] = t[8:16]

    pack(zsend)
    for side in range(2):
        ysend[side, FD] = (
            E[pl.ds(face(side), BX, stride=BY), :] * G[pl.ds(face(side), BX, stride=BY), :]
        )

    pl.semaphore_wait(barrier, len(partners))

    def remote(src, dst, a, b, dev):
        return pltpu.make_async_remote_copy(
            src_ref=src, dst_ref=dst, send_sem=a, recv_sem=b, device_id=dev, device_id_type=MESH
        )

    def ycopy(side, f):
        return remote(
            ysend.at[side, f], yrecv.at[1 - side, f], ys.at[side, f], yr.at[1 - side, f],
            ylow if side == 0 else yhigh,
        )

    def yhas(side):
        return has_ylo if side == 0 else has_yhi

    def xcopy(side):
        r = BY if side == 0 else ROWS
        return remote(
            V.at[:, pl.ds(r, BY), :], xrecv.at[1 - side], xs.at[side], xr.at[1 - side],
            xlow if side == 0 else xhigh,
        )

    def xhas(side):
        return has_xlo if side == 0 else has_xhi

    def zcopy(side, src, dst, a, b):
        return remote(
            src.at[side], dst.at[1 - side], a.at[side], b.at[1 - side],
            zlow if side == 0 else zhigh,
        )

    def when_each(has, fn):
        for side in range(2):
            pl.when(has(side))(lambda side=side: fn(side))

    def send_y(side, fields):
        for f in fields:
            ycopy(side, f).start()

    when_each(yhas, lambda side: send_y(side, (FVZ,)))
    for side in range(2):
        zcopy(side, zsend, zrecv, zs, zr).start()
    when_each(xhas, lambda side: xcopy(side).start())
    when_each(yhas, lambda side: send_y(side, (FVY, FP, FVX, FD)))

    def not_(has):
        return lambda side: jnp.logical_not(has(side))

    def wall_y(side):
        for f in (FVZ, FVY, FVX, FD, FC):
            yrecv[side, f] = jnp.zeros((BX, BZ), jnp.float32)
        yrecv[side, FP] = V[PR, pl.ds(BY + face(side), BX, stride=BY), :]

    def wall_x(side):
        for f in (VX, VY, VZ):
            xrecv[side, f] = zero
        xrecv[side, PR] = V[PR, pl.ds(BY if side == 0 else ROWS, BY), :]
        FX[pl.ds(0 if side == 0 else ROWS + BY, BY), :] = zero

    when_each(not_(yhas), wall_y)
    when_each(not_(xhas), wall_x)

    when_each(xhas, lambda side: xcopy(1 - side).wait_recv())
    for side in range(2):
        sg = 0.5 if side == 0 else -0.5
        r = BY if side == 0 else ROWS
        g = G[pl.ds(r - BY, BY), :]
        coef = NU + sg * V[VX, pl.ds(r, BY), :]
        for k in range(3):
            n = coef * xrecv[side, k]
            if k == 0:
                n = n + sg * xrecv[side, PR]
            vel_o[k, pl.ds(r - BY, BY), :] += g * n

    for side in range(2):
        zcopy(1 - side, zsend, zrecv, zs, zr).wait_recv()
    for i in range(4):
        ln = pl.ds(BZ * i, BZ)
        vlo, vhi = zsend[0, 2:3, ln], zsend[1, 2:3, ln]
        clo, chi = NU + 0.5 * vlo, NU - 0.5 * vhi
        for k in range(3):
            nlo, nhi = clo * zrecv[0, k:k + 1, ln], chi * zrecv[1, k:k + 1, ln]
            if k == 2:
                nlo = nlo + 0.5 * zrecv[0, 3:4, ln]
                nhi = nhi - 0.5 * zrecv[1, 3:4, ln]
            Q[2 * k:2 * k + 1, ln] = nhi
            Q[2 * k + 1:2 * k + 2, ln] = nlo
        Q[6:7, ln] = zrecv[1, 4:5, ln]
        Q[7:8, ln] = zrecv[0, 4:5, ln]

    def unpack():
        for i in range(4):
            S[pl.ds(BZ * i, BZ), :] = Q[:, pl.ds(BZ * i, BZ)].T

    unpack()
    edge = (lane == 0) | (lane == BZ - 1)

    def zfix(x, carry):
        flow, void = carry
        o = pl.multiple_of(x * BY, BY)
        q, g, e = S[pl.ds(o, BY), :], G[pl.ds(o, BY), :], E[pl.ds(o, BY), :]
        for k in range(3):
            u = vel_o[k, pl.ds(o, BY), :] + g * jnp.where(edge, pltpu.roll(q, BZ - 1 - 2 * k, 1), 0.0)
            vel_o[k, pl.ds(o, BY), :] = u
        h = pltpu.roll(q, BZ - 7, 1)
        SL[pl.ds(o, BY), :] = 0.5 * (
            jnp.where(lane == BZ - 1, h, pltpu.roll(e, BZ - 1, 1))
            - jnp.where(lane == 0, h, pltpu.roll(e, 1, 1))
        )
        return flow + e * u, void + e

    flow, void = lax.fori_loop(0, BX, zfix, (zero, zero))

    def send_c(side):
        ycopy(side, FC).start()

    for side in range(2):
        ysend[side, FC] = (
            E[pl.ds(face(side), BX, stride=BY), :] * vel_o[VY, pl.ds(face(side), BX, stride=BY), :]
        )
    when_each(yhas, send_c)

    def ywait(side, fields):
        for f in fields:
            ycopy(1 - side, f).wait_recv()

    def yfix(side, k, f):
        sg = 0.5 if side == 0 else -0.5
        rows = pl.ds(face(side), BX, stride=BY)
        n = (NU + sg * ysend[side, FVY]) * yrecv[side, f]
        if k == VY:
            n = n + sg * yrecv[side, FP]
        g = G[rows, :]
        vel_o[k, rows, :] = vel_o[k, rows, :] + g * n
        return n

    when_each(yhas, lambda side: ywait(side, (FVZ,)))
    ysum = jnp.zeros((BX, BZ), jnp.float32)
    for side in range(2):
        ysum = ysum + ysend[side, FD] * yfix(side, VZ, FVZ)

    def spread(a, b):
        a, b = jnp.sum(a, axis=0, keepdims=True), jnp.sum(b, axis=0, keepdims=True)
        return jnp.where(
            lane[0:1] < BZ // 2, a + pltpu.roll(a, BZ // 2, 1), b + pltpu.roll(b, BZ // 2, 1)
        )

    part = spread(flow + (ysum[0:16] + ysum[16:32]), void)
    row1[0] = part
    red1[zabs] = part

    def c1(k):
        return remote(row1.at[0], red1.at[zabs], s1.at[k], r1.at[k], zpeers[k - 1])

    def c2(k):
        return remote(row2.at[0], red2.at[plane], s2.at[k], r2.at[k], ppeers[k - 1])

    for k in range(1, 16):
        c1(k).start()

    when_each(yhas, lambda side: ywait(side, (FVY, FP, FVX)))
    for side in range(2):
        yfix(side, VY, FVY)
        yfix(side, VX, FVX)

    def fluxes(x, carry):
        o = pl.multiple_of(x * BY, BY)
        e = E[pl.ds(o, BY), :]
        FX[pl.ds(o + BY, BY), :] = e * vel_o[VX, pl.ds(o, BY), :]
        fz = e * vel_o[VZ, pl.ds(o, BY), :]
        S[pl.ds(o, BY), :] = jnp.where(lane == 8, pltpu.roll(fz, 9, 1), fz)
        return carry

    lax.fori_loop(0, BX, fluxes, 0)
    for side in range(2):
        xsend2[side] = FX[pl.ds(BY if side == 0 else ROWS, BY), :]
    pack(zsend2)

    def xcopy2(side):
        return remote(
            xsend2.at[side], FX.at[pl.ds(ROWS + BY if side == 0 else 0, BY), :],
            xs2.at[side], xr2.at[1 - side], xlow if side == 0 else xhigh,
        )

    when_each(xhas, lambda side: xcopy2(side).start())
    for side in range(2):
        zcopy(side, zsend2, zrecv2, zs2, zr2).start()

    for k in range(1, 16):
        c1(k).wait_recv()
    part2 = red1[0]
    for i in range(1, 16):
        part2 = part2 + red1[i]
    row2[0] = part2
    red2[plane] = part2
    for k in range(1, 32):
        c2(k).start()

    when_each(yhas, lambda side: ywait(side, (FD, FC)))
    for side in range(2):
        sg = -0.5 if side == 0 else 0.5
        n = (NU + sg * yrecv[side, FVY]) * ysend[side, FVY] + sg * ysend[side, FP]
        yrecv[side, FC] = yrecv[side, FC] + yrecv[side, FD] * n

    for side in range(2):
        zcopy(1 - side, zsend2, zrecv2, zs2, zr2).wait_recv()
    Q[0:1, :] = zrecv2[1, 0:1, :]
    Q[1:2, :] = zrecv2[0, 0:1, :]
    unpack()
    when_each(xhas, lambda side: xcopy2(1 - side).wait_recv())

    def diverge(x, carry):
        o = pl.multiple_of(x * BY, BY)
        e = E[pl.ds(o, BY), :]
        fy = e * vel_o[VY, pl.ds(o, BY), :]
        fz = e * vel_o[VZ, pl.ds(o, BY), :]
        h = pltpu.roll(S[pl.ds(o, BY), :], BZ - 1, 1)
        d = FX[pl.ds(o + 2 * BY, BY), :] - FX[pl.ds(o, BY), :]
        d = d + (
            jnp.where(rown == BY - 1, yrecv[1, FC, pl.ds(x, 1), :], pltpu.roll(fy, BY - 1, 0))
            - jnp.where(rown == 0, yrecv[0, FC, pl.ds(x, 1), :], pltpu.roll(fy, 1, 0))
        )
        d = d + (
            jnp.where(lane == BZ - 1, h, pltpu.roll(fz, BZ - 1, 1))
            - jnp.where(lane == 0, h, pltpu.roll(fz, 1, 1))
        )
        src_o[pl.ds(o, BY), :] = 0.5 * d
        return carry

    lax.fori_loop(0, BX, diverge, 0)

    for k in range(1, 32):
        c2(k).wait_recv()
    total = red2[0]
    for i in range(1, 32):
        total = total + red2[i]
    half = lane[0:1] < BZ // 2
    flow_sum = jnp.sum(jnp.where(half, total, 0.0), axis=1, keepdims=True)
    void_sum = jnp.sum(jnp.where(half, 0.0, total), axis=1, keepdims=True)
    cells = float(ROWS * BZ * 512)
    step = (target_ref[0] * cells - flow_sum) / (DT * void_sum)
    force_o[...] = force + step
    add = jnp.broadcast_to(DT * step, (BY, BZ))

    def finish(x, carry):
        o = pl.multiple_of(x * BY, BY)
        vel_o[VZ, pl.ds(o, BY), :] += add
        src_o[pl.ds(o, BY), :] += add * SL[pl.ds(o, BY), :]
        return carry

    lax.fori_loop(0, BX, finish, 0)

    when_each(yhas, lambda side: [ycopy(side, f).wait_send() for f in range(6)] and None)
    when_each(xhas, lambda side: (xcopy(side).wait_send(), xcopy2(side).wait_send()) and None)
    for side in range(2):
        zcopy(side, zsend, zrecv, zs, zr).wait_send()
        zcopy(side, zsend2, zrecv2, zs2, zr2).wait_send()
    for k in range(1, 16):
        c1(k).wait_send()
    for k in range(1, 32):
        c2(k).wait_send()


def local(velocity, pressure, voidage, particle_vel, forcing, target_flux):
    f32 = jnp.float32
    vmem = pl.BlockSpec(memory_space=pltpu.VMEM)
    smem = pl.BlockSpec(memory_space=pltpu.SMEM)
    hbm = pl.BlockSpec(memory_space=pl.ANY)
    dma = pltpu.SemaphoreType.DMA
    vel, src, force = pl.pallas_call(
        kernel,
        out_shape=(
            jax.ShapeDtypeStruct((3, ROWS, BZ), f32),
            jax.ShapeDtypeStruct((ROWS, BZ), f32),
            jax.ShapeDtypeStruct((1, 1), f32),
        ),
        in_specs=[smem, smem, hbm, hbm, hbm, hbm],
        out_specs=(vmem, vmem, vmem),
        scratch_shapes=[
            pltpu.VMEM((4, PAD, BZ), f32),
            pltpu.VMEM((ROWS, BZ), f32),
            pltpu.VMEM((3, ROWS, BZ), f32),
            pltpu.VMEM((ROWS, BZ), f32),
            pltpu.VMEM((ROWS, BZ), f32),
            pltpu.VMEM((ROWS, BZ), f32),
            pltpu.VMEM((PAD, BZ), f32),
            pltpu.VMEM((BZ, ROWS), f32),
            pltpu.VMEM((2, 4, BY, BZ), f32),
            pltpu.VMEM((2, 8, ROWS), f32),
            pltpu.VMEM((2, 8, ROWS), f32),
            pltpu.VMEM((2, 8, ROWS), f32),
            pltpu.VMEM((2, 8, ROWS), f32),
            pltpu.VMEM((2, 6, BX, BZ), f32),
            pltpu.VMEM((2, 6, BX, BZ), f32),
            pltpu.VMEM((2, BY, BZ), f32),
            pltpu.VMEM((1, 1, BZ), f32),
            pltpu.VMEM((16, 1, BZ), f32),
            pltpu.VMEM((1, 1, BZ), f32),
            pltpu.VMEM((32, 1, BZ), f32),
            dma((4,)), dma((2,)), dma((2,)), dma((2,)), dma((2,)), dma((2,)), dma((2,)),
            dma((2, 6)), dma((2, 6)), dma((2,)), dma((2,)),
            dma((16,)), dma((16,)), dma((32,)), dma((32,)),
        ],
        compiler_params=pltpu.CompilerParams(collective_id=0, has_side_effects=True),
    )(
        forcing,
        target_flux,
        velocity.reshape(3, ROWS, BZ),
        pressure.reshape(ROWS, BZ),
        voidage.reshape(ROWS, BZ),
        particle_vel.reshape(3, ROWS, BZ),
    )
    return vel.reshape(3, BX, BY, BZ), src.reshape(BX, BY, BZ), force.reshape(1)


def solution(mesh):
    return jax.shard_map(
        local,
        mesh=mesh,
        in_specs=(
            P(None, "gx", "gy", "gz"), P("gx", "gy", "gz"), P("gx", "gy", "gz"),
            P(None, "gx", "gy", "gz"), P(), P(),
        ),
        out_specs=(P(None, "gx", "gy", "gz"), P("gx", "gy", "gz"), P()),
        check_vma=False,
    )
```

time: 168 us -> 56.7 us (0.34)
  the two profiles are of different devices: /device:TPU:32 before, /device:TPU:1 now
where the time goes in v1:
time: 56.7 us; the launch traced here: 56.3 us
  Pallas kernels  49.8 us (88%)
  between operations  3.7 us (7%)
  local copies, waits for them, and re-layouts  2.81 us (5%)
    pallas_call x1, Pallas kernels, local(): pl.pallas_call(kernel, out_shape=(jax.ShapeDtypeStruct((3, ROWS, BZ), f32...  49.8 us
    unnamed x4, local copies, waits for them, and re-layouts  2.81 us

profile of v1, /device:TPU:1, one launch (start us, length us, event | category | flops | bytes accessed | tf_op | source)
XLA Modules:
  0.0 56.3 jit_solution(16831563834648430644)
XLA Ops:
  1.9 49.8 %shard_map.85 = (f32[3,512,128]{2,1,0:T(8,128)}, f32[512,128]{1,0:T(8,128)}, f32[1,1]{1,0:T(1,128)}) custom-call(f32[1]{0:T(128)S(6)} %copy.12.force_ref, f32[1]{0:T(128)S(6)} %copy.13.target_ref, f32[3,512,128]{2,1,0:T(8,128)} %bitcast.8, f32[512,128]{1,0:T(8,128)} %bitcast.11, f32[512,128]{1,0:T(8,128)} %bitcast.12, f32[3,512,128]{2,1,0:T(8,128)} %bitcast.9), custom_call_target="tpu_custom_call" | custom-call | tf_op jit(solution)/shard_map/pallas_call | solution.py:406
  51.7 0.0 copy-start
  51.7 2.1 %copy.14 = f32[3,32,16,128]{3,2,1,0:T(8,128)} copy(f32[3,32,16,128]{3,2,1,0:T(8,128)} %bitcast.7) | data formatting | bytes 1572864
  53.8 0.0 copy-done
  53.8 0.7 %copy.15 = f32[32,16,128]{2,1,0:T(8,128)} copy(f32[32,16,128]{2,1,0:T(8,128)S(1)} %bitcast.10) | data formatting | bytes 524288
Async XLA Ops:
  51.7 2.1 %copy-start = (f32[512,128]{1,0:T(8,128)S(1)}, f32[512,128]{1,0:T(8,128)}, u32[]{:S(2)}) copy-start(f32[512,128]{1,0:T(8,128)} %get-tuple-element.7) | copy-start | bytes 786436

commit v2 on v1

--- a/solution.py
+++ b/solution.py
@@ -16,9 +16,9 @@
 
 
 def kernel(
-    force_ref, target_ref, vel_h, pres_h, eps_h, pv_h,
-    vel_o, src_o, force_o,
-    V, E, PV, G, S, SL, FX, Q,
+    force_h, target_h, vel_h, pres_h, eps_h, pv_h,
+    vel_o, src_o, SL, aux_o,
+    V, E, PV, G, S, FX, Q, scal,
     xrecv, zsend, zrecv, zsend2, zrecv2, ysend, yrecv, xsend2,
     row1, red1, row2, red2,
     lsem, xs, xr, zs, zr, zs2, zr2, ys, yr, xs2, xr2, s1, r1, s2, r2,
@@ -60,6 +60,8 @@
         pltpu.make_async_copy(pres_h, V.at[3, pl.ds(BY, ROWS), :], lsem.at[1]),
         pltpu.make_async_copy(eps_h, E, lsem.at[2]),
         pltpu.make_async_copy(pv_h, PV, lsem.at[3]),
+        pltpu.make_async_copy(force_h, scal.at[0], lsem.at[4]),
+        pltpu.make_async_copy(target_h, scal.at[1], lsem.at[5]),
     ]
     for cp in loads:
         cp.start()
@@ -71,9 +73,9 @@
         V[f, pl.ds(0, BY), :] = zero
         V[f, pl.ds(ROWS + BY, BY), :] = zero
     Q[...] = jnp.zeros_like(Q)
-    force = force_ref[0]
     for cp in loads:
         cp.wait()
+    force, target = scal[0, 0], scal[1, 0]
 
     def face(side):
         return 0 if side == 0 else BY - 1
@@ -374,17 +376,9 @@
     flow_sum = jnp.sum(jnp.where(half, total, 0.0), axis=1, keepdims=True)
     void_sum = jnp.sum(jnp.where(half, 0.0, total), axis=1, keepdims=True)
     cells = float(ROWS * BZ * 512)
-    step = (target_ref[0] * cells - flow_sum) / (DT * void_sum)
-    force_o[...] = force + step
-    add = jnp.broadcast_to(DT * step, (BY, BZ))
-
-    def finish(x, carry):
-        o = pl.multiple_of(x * BY, BY)
-        vel_o[VZ, pl.ds(o, BY), :] += add
-        src_o[pl.ds(o, BY), :] += add * SL[pl.ds(o, BY), :]
-        return carry
-
-    lax.fori_loop(0, BX, finish, 0)
+    step = (target * cells - flow_sum) / (DT * void_sum)
+    aux_o[0:1, :] = jnp.broadcast_to(DT * step, (1, BZ))
+    aux_o[1:2, :] = jnp.broadcast_to(force + step, (1, BZ))
 
     when_each(yhas, lambda side: [ycopy(side, f).wait_send() for f in range(6)] and None)
     when_each(xhas, lambda side: (xcopy(side).wait_send(), xcopy2(side).wait_send()) and None)
@@ -397,30 +391,47 @@
         c2(k).wait_send()
 
 
+def finish(vel, src, slope, aux, vel_o, src_o, force_o, vz, out, sem):
+    pairs = [
+        pltpu.make_async_copy(vel.at[pl.ds(0, 2)], vel_o.at[pl.ds(0, 2)], sem.at[0]),
+        pltpu.make_async_copy(vz, vel_o.at[VZ], sem.at[1]),
+        pltpu.make_async_copy(out, src_o, sem.at[2]),
+    ]
+    pairs[0].start()
+    force_o[...] = aux[1:2, 0:1]
+    add = aux[0:1, :]
+    vz[...] = vel[VZ] + add
+    pairs[1].start()
+    out[...] = src[...] + add * slope[...]
+    pairs[2].start()
+    for cp in pairs:
+        cp.wait()
+
+
 def local(velocity, pressure, voidage, particle_vel, forcing, target_flux):
     f32 = jnp.float32
     vmem = pl.BlockSpec(memory_space=pltpu.VMEM)
-    smem = pl.BlockSpec(memory_space=pltpu.SMEM)
     hbm = pl.BlockSpec(memory_space=pl.ANY)
     dma = pltpu.SemaphoreType.DMA
-    vel, src, force = pl.pallas_call(
+    parts = pl.pallas_call(
         kernel,
         out_shape=(
-            jax.ShapeDtypeStruct((3, ROWS, BZ), f32),
-            jax.ShapeDtypeStruct((ROWS, BZ), f32),
-            jax.ShapeDtypeStruct((1, 1), f32),
+            pltpu.VMEM((3, ROWS, BZ), f32),
+            pltpu.VMEM((ROWS, BZ), f32),
+            pltpu.VMEM((ROWS, BZ), f32),
+            pltpu.VMEM((8, BZ), f32),
         ),
-        in_specs=[smem, smem, hbm, hbm, hbm, hbm],
-        out_specs=(vmem, vmem, vmem),
+        in_specs=[pl.BlockSpec(memory_space=pltpu.HBM)] * 6,
+        out_specs=(vmem,) * 4,
         scratch_shapes=[
             pltpu.VMEM((4, PAD, BZ), f32),
             pltpu.VMEM((ROWS, BZ), f32),
             pltpu.VMEM((3, ROWS, BZ), f32),
             pltpu.VMEM((ROWS, BZ), f32),
             pltpu.VMEM((ROWS, BZ), f32),
-            pltpu.VMEM((ROWS, BZ), f32),
             pltpu.VMEM((PAD, BZ), f32),
             pltpu.VMEM((BZ, ROWS), f32),
+            pltpu.SMEM((2, 1), f32),
             pltpu.VMEM((2, 4, BY, BZ), f32),
             pltpu.VMEM((2, 8, ROWS), f32),
             pltpu.VMEM((2, 8, ROWS), f32),
@@ -433,7 +444,7 @@
             pltpu.VMEM((16, 1, BZ), f32),
             pltpu.VMEM((1, 1, BZ), f32),
             pltpu.VMEM((32, 1, BZ), f32),
-            dma((4,)), dma((2,)), dma((2,)), dma((2,)), dma((2,)), dma((2,)), dma((2,)),
+            dma((6,)), dma((2,)), dma((2,)), dma((2,)), dma((2,)), dma((2,)), dma((2,)),
             dma((2, 6)), dma((2, 6)), dma((2,)), dma((2,)),
             dma((16,)), dma((16,)), dma((32,)), dma((32,)),
         ],
@@ -446,6 +457,18 @@
         voidage.reshape(ROWS, BZ),
         particle_vel.reshape(3, ROWS, BZ),
     )
+    vel, src, force = pl.pallas_call(
+        finish,
+        out_shape=(
+            jax.ShapeDtypeStruct((3, ROWS, BZ), f32),
+            jax.ShapeDtypeStruct((ROWS, BZ), f32),
+            jax.ShapeDtypeStruct((1, 1), f32),
+        ),
+        in_specs=[vmem] * 4,
+        out_specs=(hbm, hbm, vmem),
+        scratch_shapes=[pltpu.VMEM((ROWS, BZ), f32), pltpu.VMEM((ROWS, BZ), f32), dma((3,))],
+        compiler_params=pltpu.CompilerParams(vmem_limit_bytes=8 * 1024 * 1024),
+    )(*[pltpu.with_memory_space_constraint(p, pltpu.VMEM) for p in parts])
     return vel.reshape(3, BX, BY, BZ), src.reshape(BX, BY, BZ), force.reshape(1)
 
 

time: 56.7 us -> 52.5 us (0.926)
  local copies, waits for them, and re-layouts: 2.81 us -> 0 us
  between operations: 3.7 us -> 1.93 us
    unnamed x4 -> x0, local copies, waits for them, and re-layouts: 2.81 us -> none
    pallas_call x1 -> x2, Pallas kernels: 49.8 us -> 50.1 us  [the longest x1 48.6 us: local(): pl.pallas_call(kernel, out_shape=(pltpu.VMEM((3, ROWS, BZ), f32), pltpu.V...]
where the time goes in v2:
time: 52.5 us; the launch traced here: 52 us
  Pallas kernels  50.1 us (95%)
  between operations  1.93 us (4%)
    pallas_call x1, Pallas kernels, local(): pl.pallas_call(kernel, out_shape=(pltpu.VMEM((3, ROWS, BZ), f32), pltpu.V...  48.6 us
    pallas_call x1, Pallas kernels, local(): pl.pallas_call(finish, out_shape=(jax.ShapeDtypeStruct((3, ROWS, BZ), f32...  1.5 us

profile of v2, /device:TPU:1, one launch (start us, length us, event | category | flops | bytes accessed | tf_op | source)
XLA Modules:
  0.0 52.0 jit_solution(2499985152949302090)
XLA Ops:
  1.9 48.6 %shard_map.85 = (f32[3,512,128]{2,1,0:T(8,128)S(1)}, f32[512,128]{1,0:T(8,128)S(1)}, f32[512,128]{1,0:T(8,128)S(1)}, f32[8,128]{1,0:T(8,128)S(1)}) custom-call(f32[1]{0:T(128)S(6)} %copy.9.force_h, f32[1]{0:T(128)S(6)} %copy.10.target_h, f32[3,512,128]{2,1,0:T(8,128)} %bitcast.7, f32[512,128]{1,0:T(8,128)} %bitcast.9, f32[512,128]{1,0:T(8,128)} %bitcast.10, ...), custom_call_target="tpu_custom_call" | custom-call | tf_op jit(solution)/shard_map/pallas_call | solution.py:416
  50.5 1.5 %shard_map.86 = (f32[3,512,128]{2,1,0:T(8,128)}, f32[512,128]{1,0:T(8,128)}, f32[1,1]{1,0:T(1,128)}) custom-call(f32[3,512,128]{2,1,0:T(8,128)S(1)} %get-tuple-element.10.vel, f32[512,128]{1,0:T(8,128)S(1)} %get-tuple-element.11.src, f32[512,128]{1,0:T(8,128)S(1)} %get-tuple-element.12.slope, f32[8,128]{1,0:T(8,128)S(1)} %get-tuple-element.13.aux), custom_call_target="tpu_custom_call" | custom-call | tf_op jit(solution)/shard_map/pallas_call | solution.py:460

commit v3 on v2

--- a/solution.py
+++ b/solution.py
@@ -12,16 +12,26 @@
 ROWS = BX * BY
 PAD = ROWS + 2 * BY
 VX, VY, VZ, PR = 0, 1, 2, 3
-FVZ, FVY, FP, FVX, FD, FC = 0, 1, 2, 3, 4, 5
+FVZ, FVY, FD, FP, FVX, FC = 0, 1, 2, 3, 4, 5
+GROUPS = ((0, 3), (3, 2), (5, 1))
+NZ_, NY_, NX_, NF_ = 0, 1, 2, 3
+BACK = ((0, 1), (1, 2), (3, 1))
+
+
+def weight(c, pv, e):
+    a, b, d = c[0] - pv[0], c[1] - pv[1], c[2] - pv[2]
+    slip = jnp.sqrt(a * a + b * b + d * d)
+    drag = (1.0 - e) * jnp.exp(-2.65 * jnp.log(e)) * (1.0 + slip)
+    return drag, 1.0 / (1.0 + DT * drag)
 
 
 def kernel(
     force_h, target_h, vel_h, pres_h, eps_h, pv_h,
     vel_o, src_o, SL, aux_o,
     V, E, PV, G, S, FX, Q, scal,
-    xrecv, zsend, zrecv, zsend2, zrecv2, ysend, yrecv, xsend2,
+    xrecv, zsend, zrecv, zsend2, zrecv2, ysend, yrecv, msend, mrecv, yacc, xsend2, rbuf,
     row1, red1, row2, red2,
-    lsem, xs, xr, zs, zr, zs2, zr2, ys, yr, xs2, xr2, s1, r1, s2, r2,
+    lsem, xs, xr, zs, zr, zs2, zr2, ys, yr, ms, mr, xs2, xr2, s1, r1, s2, r2, know, wave, cross, rsem, fsem,
 ):
     gz, gy, gx = lax.axis_index("gz"), lax.axis_index("gy"), lax.axis_index("gx")
     ngz, ngy, ngx = 16, 8, 4
@@ -37,23 +47,32 @@
     has_xlo, has_xhi = gx > 0, gx < ngx - 1
     has_ylo, has_yhi = gy > 0, gy < ngy - 1
 
-    def of_z(z):
-        return at(gz=lax.rem(z, 8) * 2 + core, gy=y * 2 + z // 8)
+    def of_z(z, dy=0):
+        z, yy = lax.rem(z, 16), lax.rem(y + dy + 4, 4)
+        return at(gz=lax.rem(z, 8) * 2 + core, gy=yy * 2 + z // 8)
 
     def of_plane(i):
         return at(gx=i // 8, gy=lax.rem(i // 2, 4) * 2 + zhi, gz=zlo * 2 + lax.rem(i, 2))
 
     plane = gx * 8 + y * 2 + core
-    zpeers = [of_z(lax.rem(zabs + k, 16)) for k in range(1, 16)]
+    zpeers = [of_z(zabs + k) for k in range(1, 16)]
     ppeers = [of_plane(lax.rem(plane + k, 32)) for k in range(1, 32)]
     zlow, zhigh = at(gz=lax.rem(gz + ngz - 1, ngz)), at(gz=lax.rem(gz + 1, ngz))
-    ylow, yhigh = at(gy=lax.rem(gy + ngy - 1, ngy)), at(gy=lax.rem(gy + 1, ngy))
     xlow, xhigh = at(gx=lax.rem(gx + ngx - 1, ngx)), at(gx=lax.rem(gx + 1, ngx))
 
     barrier = pltpu.get_barrier_semaphore()
-    partners = [ylow, yhigh] + zpeers + [zlow, zhigh] + ppeers
-    for d in partners:
+    below, above = [of_z(zabs + 16 - k) for k in (1, 2, 4)], [of_z(zabs + k) for k in (1, 2, 4)]
+    yprev, ynext = of_z(zabs, -1), of_z(zabs, 1)
+    other = at(gz=zlo * 2 + 1 - core)
+    outer_far = (gz == 0) | (gz == ngz - 1)
+    outer = at(gz=lax.rem(gz + ngz - 1 + 2 * core, ngz))
+    nearest = [below[0], above[0], other, xlow, xhigh, yprev, ynext]
+    for d in nearest:
         pl.semaphore_signal(barrier, inc=1, device_id=d, device_id_type=MESH)
+
+    @pl.when(jnp.logical_not(outer_far))
+    def _():
+        pl.semaphore_signal(barrier, inc=1, device_id=outer, device_id_type=MESH)
 
     loads = [
         pltpu.make_async_copy(vel_h, V.at[pl.ds(0, 3), pl.ds(BY, ROWS), :], lsem.at[0]),
@@ -73,6 +92,26 @@
         V[f, pl.ds(0, BY), :] = zero
         V[f, pl.ds(ROWS + BY, BY), :] = zero
     Q[...] = jnp.zeros_like(Q)
+    def tell(step):
+        pl.semaphore_signal(know.at[step, 0], inc=1, device_id=above[step], device_id_type=MESH)
+        pl.semaphore_signal(know.at[step, 1], inc=1, device_id=below[step], device_id_type=MESH)
+
+    def heard(step, side):
+        pl.semaphore_wait(know.at[step, side], 1)
+
+    waves = [(xlow, xhigh), (yprev, ynext), (yprev, ynext), (other,)]
+
+    def plane_tell(i):
+        for d in waves[i]:
+            pl.semaphore_signal(wave.at[i], inc=1, device_id=d, device_id_type=MESH)
+
+    def plane_heard(i):
+        pl.semaphore_wait(wave.at[i], len(waves[i]))
+
+    pl.semaphore_wait(barrier, len(nearest) + jnp.where(outer_far, 0, 1))
+    tell(0)
+    plane_tell(0)
+
     for cp in loads:
         cp.wait()
     force, target = scal[0, 0], scal[1, 0]
@@ -81,8 +120,138 @@
         return 0 if side == 0 else BY - 1
 
     for side in range(2):
-        for slot, f in ((FVZ, VZ), (FVY, VY), (FP, PR), (FVX, VX)):
-            ysend[side, slot] = V[f, pl.ds(BY + face(side), BX, stride=BY), :]
+        rows = pl.ds(face(side), BX, stride=BY)
+        v = [V[f, pl.ds(BY + face(side), BX, stride=BY), :] for f in range(4)]
+        ysend[side, FVZ], ysend[side, FVY] = v[VZ], v[VY]
+        ysend[side, FP], ysend[side, FVX] = v[PR], v[VX]
+        e = E[rows, :]
+        ysend[side, FD] = e * DT * weight(v, [PV[k, rows, :] for k in range(3)], e)[1]
+
+    heard(0, 0)
+    heard(0, 1)
+    tell(1)
+
+    def remote(src, dst, a, b, dev):
+        return pltpu.make_async_remote_copy(
+            src_ref=src, dst_ref=dst, send_sem=a, recv_sem=b, device_id=dev, device_id_type=MESH
+        )
+
+    def side_of(kind):
+        return 1 - zhi if kind == 0 else zhi
+
+    def ycopy(kind, j):
+        side, part = side_of(kind), pl.ds(*GROUPS[j])
+        return remote(
+            ysend.at[side, part], mrecv.at[1 - side, part], ys.at[kind, j], mr.at[1 - side, j],
+            of_z(zabs + 12 + 8 * side, kind * zhi),
+        )
+
+    def paired(kind):
+        return (gy >= 0) if kind == 0 else jnp.where(zhi == 0, y, 3 - y) > 0
+
+    def mwait(q, j):
+        part = pl.ds(*GROUPS[j])
+        remote(ysend.at[0, part], mrecv.at[q, part], ys.at[0, j], mr.at[q, j], above[2]).wait_recv()
+
+    def yhas(side):
+        return has_ylo if side == 0 else has_yhi
+
+    intra = (zabs >= 4) & (zabs < 12)
+    middle = intra | (y > 0)
+
+    def mcopy(q, j):
+        part = pl.ds(*BACK[j])
+        return remote(
+            msend.at[q, part], yrecv.at[1 - q, part], ms.at[q, j], yr.at[1 - q, j],
+            of_z(zabs + 12, jnp.where(intra, 0, -1)) if q == 0 else of_z(zabs + 4),
+        )
+
+    def xcopy(side):
+        r = BY if side == 0 else ROWS
+        return remote(
+            V.at[:, pl.ds(r, BY), :], xrecv.at[1 - side], xs.at[side], xr.at[1 - side],
+            xlow if side == 0 else xhigh,
+        )
+
+    def xhas(side):
+        return has_xlo if side == 0 else has_xhi
+
+    def zcopy(side, src, dst, a, b):
+        return remote(
+            src.at[side], dst.at[1 - side], a.at[side], b.at[1 - side],
+            zlow if side == 0 else zhigh,
+        )
+
+    def when_each(has, fn):
+        for side in range(2):
+            pl.when(has(side))(lambda side=side: fn(side))
+
+    def send_y(kind, groups):
+        @pl.when(paired(kind))
+        def _():
+            for g in groups:
+                ycopy(kind, g).start()
+
+    when_each(xhas, lambda side: xcopy(side).start())
+    plane_heard(0)
+    plane_tell(1)
+
+    def columns(x, carry):
+        o = pl.multiple_of(x * BY, BY)
+        s = zero
+        for k, a in enumerate([V[f, pl.ds(o + BY, BY), :] for f in range(4)] + [E[pl.ds(o, BY), :]]):
+            s = jnp.where(lane == k, a if k == 0 else pltpu.roll(a, k, 1), s)
+            s = jnp.where(lane == 8 + k, pltpu.roll(a, 9 + k, 1), s)
+        S[pl.ds(o, BY), :] = s
+        return carry
+
+    lax.fori_loop(0, BX, columns, 0, unroll=4)
+
+    def pack(dst):
+        for i in range(4):
+            t = S[pl.ds(BZ * i, BZ), :].T
+            dst[0, :, pl.ds(BZ * i, BZ)] = t[0:8]
+            dst[1, :, pl.ds(BZ * i, BZ)] = t[8:16]
+
+    pack(zsend)
+    relay = zlo == 4 - core
+
+    def zwrap():
+        return remote(
+            zsend.at[core], rbuf, zs.at[core], rsem, of_z(zabs + 20 - 8 * core),
+        )
+
+    def zforward():
+        return remote(
+            rbuf, zrecv.at[1 - core], fsem, zr.at[1 - core], at(gz=gz + 7 - 14 * core),
+        )
+
+    for side in range(2):
+        @pl.when(jnp.logical_not(outer_far & (core == side)))
+        def _():
+            zcopy(side, zsend, zrecv, zs, zr).start()
+
+    heard(1, 1 - zhi)
+    send_y(0, (0,))
+    heard(1, zhi)
+
+    tell(2)
+
+    @pl.when(outer_far)
+    def _():
+        zwrap().start()
+
+    @pl.when(zhi == 1)
+    def _():
+        pl.semaphore_signal(
+            cross, inc=1, device_id=of_z(zabs, -1), device_id_type=MESH
+        )
+        pl.semaphore_wait(cross, 1)
+
+    send_y(1, (0,))
+
+    plane_heard(1)
+    plane_tell(2)
 
     def slab(x, carry):
         o = pl.multiple_of(x * BY, BY)
@@ -95,13 +264,7 @@
         zp = [jnp.where(lane == BZ - 1, 0.0, pltpu.roll(a, BZ - 1, 1)) for a in c]
         ym = [jnp.where(rown == 0, 0.0, pltpu.roll(a, 1, 0)) for a in c]
         yp = [jnp.where(rown == BY - 1, 0.0, pltpu.roll(a, BY - 1, 0)) for a in c]
-        slip = jnp.sqrt(
-            (c[0] - pv[0]) * (c[0] - pv[0])
-            + (c[1] - pv[1]) * (c[1] - pv[1])
-            + (c[2] - pv[2]) * (c[2] - pv[2])
-        )
-        drag = (1.0 - e) * jnp.exp(-2.65 * jnp.log(e)) * (1.0 + slip)
-        w = 1.0 / (1.0 + DT * drag)
+        drag, w = weight(c, pv, e)
         hi, lo = (xp, yp, zp), (xm, ym, zm)
         for k in range(3):
             adv = zero
@@ -114,80 +277,27 @@
                 fk = fk + force
             vel_o[k, pl.ds(o, BY), :] = (c[k] + DT * (fk + drag * pv[k])) * w
         G[pl.ds(o, BY), :] = DT * w
-        s = zero
-        for k, a in enumerate(c + [e]):
-            s = jnp.where(lane == k, a if k == 0 else pltpu.roll(a, k, 1), s)
-            s = jnp.where(lane == 8 + k, pltpu.roll(a, 9 + k, 1), s)
-        S[pl.ds(o, BY), :] = s
         return carry
 
-    lax.fori_loop(0, BX, slab, 0)
-
-    def pack(dst):
-        for i in range(4):
-            t = S[pl.ds(BZ * i, BZ), :].T
-            dst[0, :, pl.ds(BZ * i, BZ)] = t[0:8]
-            dst[1, :, pl.ds(BZ * i, BZ)] = t[8:16]
-
-    pack(zsend)
-    for side in range(2):
-        ysend[side, FD] = (
-            E[pl.ds(face(side), BX, stride=BY), :] * G[pl.ds(face(side), BX, stride=BY), :]
-        )
-
-    pl.semaphore_wait(barrier, len(partners))
-
-    def remote(src, dst, a, b, dev):
-        return pltpu.make_async_remote_copy(
-            src_ref=src, dst_ref=dst, send_sem=a, recv_sem=b, device_id=dev, device_id_type=MESH
-        )
-
-    def ycopy(side, f):
-        return remote(
-            ysend.at[side, f], yrecv.at[1 - side, f], ys.at[side, f], yr.at[1 - side, f],
-            ylow if side == 0 else yhigh,
-        )
-
-    def yhas(side):
-        return has_ylo if side == 0 else has_yhi
-
-    def xcopy(side):
-        r = BY if side == 0 else ROWS
-        return remote(
-            V.at[:, pl.ds(r, BY), :], xrecv.at[1 - side], xs.at[side], xr.at[1 - side],
-            xlow if side == 0 else xhigh,
-        )
-
-    def xhas(side):
-        return has_xlo if side == 0 else has_xhi
-
-    def zcopy(side, src, dst, a, b):
-        return remote(
-            src.at[side], dst.at[1 - side], a.at[side], b.at[1 - side],
-            zlow if side == 0 else zhigh,
-        )
-
-    def when_each(has, fn):
-        for side in range(2):
-            pl.when(has(side))(lambda side=side: fn(side))
-
-    def send_y(side, fields):
-        for f in fields:
-            ycopy(side, f).start()
-
-    when_each(yhas, lambda side: send_y(side, (FVZ,)))
-    for side in range(2):
-        zcopy(side, zsend, zrecv, zs, zr).start()
-    when_each(xhas, lambda side: xcopy(side).start())
-    when_each(yhas, lambda side: send_y(side, (FVY, FP, FVX, FD)))
+    lax.fori_loop(0, BX, slab, 0, unroll=4)
+    send_y(0, (1,))
+    send_y(1, (1,))
+    plane_heard(2)
+    plane_tell(3)
+
+    @pl.when(relay)
+    def _():
+        zwrap().wait_recv()
+        zforward().start()
 
     def not_(has):
         return lambda side: jnp.logical_not(has(side))
 
     def wall_y(side):
-        for f in (FVZ, FVY, FVX, FD, FC):
+        sg = 0.5 if side == 0 else -0.5
+        for f in (NZ_, NX_, NF_):
             yrecv[side, f] = jnp.zeros((BX, BZ), jnp.float32)
-        yrecv[side, FP] = V[PR, pl.ds(BY + face(side), BX, stride=BY), :]
+        yrecv[side, NY_] = sg * ysend[side, FP]
 
     def wall_x(side):
         for f in (VX, VY, VZ):
@@ -247,35 +357,33 @@
         )
         return flow + e * u, void + e
 
-    flow, void = lax.fori_loop(0, BX, zfix, (zero, zero))
-
-    def send_c(side):
-        ycopy(side, FC).start()
-
-    for side in range(2):
-        ysend[side, FC] = (
-            E[pl.ds(face(side), BX, stride=BY), :] * vel_o[VY, pl.ds(face(side), BX, stride=BY), :]
-        )
-    when_each(yhas, send_c)
-
-    def ywait(side, fields):
-        for f in fields:
-            ycopy(1 - side, f).wait_recv()
-
-    def yfix(side, k, f):
-        sg = 0.5 if side == 0 else -0.5
+    flow, void = lax.fori_loop(0, BX, zfix, (zero, zero), unroll=4)
+
+    for side in range(2):
         rows = pl.ds(face(side), BX, stride=BY)
-        n = (NU + sg * ysend[side, FVY]) * yrecv[side, f]
-        if k == VY:
-            n = n + sg * yrecv[side, FP]
-        g = G[rows, :]
-        vel_o[k, rows, :] = vel_o[k, rows, :] + g * n
-        return n
-
-    when_each(yhas, lambda side: ywait(side, (FVZ,)))
-    ysum = jnp.zeros((BX, BZ), jnp.float32)
-    for side in range(2):
-        ysum = ysum + ysend[side, FD] * yfix(side, VZ, FVZ)
+        ysend[side, FC] = E[rows, :] * vel_o[VY, rows, :]
+    send_y(0, (2,))
+    send_y(1, (2,))
+
+    yacc[...] = jnp.zeros_like(yacc)
+
+    def couple(k, f, n):
+        for q in range(2):
+            sg = -0.5 if q == 0 else 0.5
+            t = (NU + sg * mrecv[q, FVY]) * mrecv[1 - q, f]
+            if k == VY:
+                t = t + sg * mrecv[1 - q, FP]
+            msend[q, n] = t
+
+    def both(fn):
+        for q in range(2):
+            fn(q)
+
+    @pl.when(middle)
+    def _():
+        both(lambda q: mwait(q, 0))
+        couple(VZ, FVZ, NZ_)
+        yacc[...] = mrecv[0, FD] * msend[0, NZ_] + mrecv[1, FD] * msend[1, NZ_]
 
     def spread(a, b):
         a, b = jnp.sum(a, axis=0, keepdims=True), jnp.sum(b, axis=0, keepdims=True)
@@ -283,63 +391,87 @@
             lane[0:1] < BZ // 2, a + pltpu.roll(a, BZ // 2, 1), b + pltpu.roll(b, BZ // 2, 1)
         )
 
-    part = spread(flow + (ysum[0:16] + ysum[16:32]), void)
+    part = spread(flow + (yacc[0:16] + yacc[16:32]), void)
     row1[0] = part
     red1[zabs] = part
 
     def c1(k):
-        return remote(row1.at[0], red1.at[zabs], s1.at[k], r1.at[k], zpeers[k - 1])
+        return remote(row1.at[0], red1.at[zabs], s1, r1, zpeers[k - 1])
 
     def c2(k):
-        return remote(row2.at[0], red2.at[plane], s2.at[k], r2.at[k], ppeers[k - 1])
-
+        return remote(row2.at[0], red2.at[plane], s2, r2, ppeers[k - 1])
+
+    heard(2, 0)
+    heard(2, 1)
     for k in range(1, 16):
         c1(k).start()
 
-    when_each(yhas, lambda side: ywait(side, (FVY, FP, FVX)))
-    for side in range(2):
-        yfix(side, VY, FVY)
-        yfix(side, VX, FVX)
-
-    def fluxes(x, carry):
+    @pl.when(middle)
+    def _():
+        both(lambda q: mcopy(q, 0).start())
+        both(lambda q: mwait(q, 1))
+        couple(VY, FVY, NY_)
+        couple(VX, FVX, NX_)
+        both(lambda q: mcopy(q, 1).start())
+        both(lambda q: mwait(q, 2))
+        for q in range(2):
+            msend[q, NF_] = mrecv[1 - q, FC] + mrecv[1 - q, FD] * msend[1 - q, NY_]
+        both(lambda q: mcopy(q, 2).start())
+
+    def yback(j, terms):
+        when_each(yhas, lambda side: mcopy(1 - side, j).wait_recv())
+        for side in range(2):
+            rows = pl.ds(face(side), BX, stride=BY)
+            g = G[rows, :]
+            for k, n in terms:
+                vel_o[k, rows, :] = vel_o[k, rows, :] + g * yrecv[side, n]
+
+    yback(0, ((VZ, NZ_),))
+
+    def zflux(x, carry):
         o = pl.multiple_of(x * BY, BY)
-        e = E[pl.ds(o, BY), :]
-        FX[pl.ds(o + BY, BY), :] = e * vel_o[VX, pl.ds(o, BY), :]
-        fz = e * vel_o[VZ, pl.ds(o, BY), :]
+        fz = E[pl.ds(o, BY), :] * vel_o[VZ, pl.ds(o, BY), :]
         S[pl.ds(o, BY), :] = jnp.where(lane == 8, pltpu.roll(fz, 9, 1), fz)
         return carry
 
-    lax.fori_loop(0, BX, fluxes, 0)
-    for side in range(2):
-        xsend2[side] = FX[pl.ds(BY if side == 0 else ROWS, BY), :]
+    lax.fori_loop(0, BX, zflux, 0, unroll=8)
     pack(zsend2)
-
-    def xcopy2(side):
-        return remote(
-            xsend2.at[side], FX.at[pl.ds(ROWS + BY if side == 0 else 0, BY), :],
-            xs2.at[side], xr2.at[1 - side], xlow if side == 0 else xhigh,
-        )
-
-    when_each(xhas, lambda side: xcopy2(side).start())
     for side in range(2):
         zcopy(side, zsend2, zrecv2, zs2, zr2).start()
 
-    for k in range(1, 16):
-        c1(k).wait_recv()
+    def all_of(red, n, a, b):
+        return remote(red.at[pl.ds(0, n)], red.at[pl.ds(0, n)], a, b, above[2])
+
+    all_of(red1, 15, s1, r1).wait_recv()
     part2 = red1[0]
     for i in range(1, 16):
         part2 = part2 + red1[i]
     row2[0] = part2
     red2[plane] = part2
+    plane_heard(3)
     for k in range(1, 32):
         c2(k).start()
 
-    when_each(yhas, lambda side: ywait(side, (FD, FC)))
-    for side in range(2):
-        sg = -0.5 if side == 0 else 0.5
-        n = (NU + sg * yrecv[side, FVY]) * ysend[side, FVY] + sg * ysend[side, FP]
-        yrecv[side, FC] = yrecv[side, FC] + yrecv[side, FD] * n
-
+    yback(1, ((VX, NX_), (VY, NY_)))
+
+    def xflux(x, carry):
+        o = pl.multiple_of(x * BY, BY)
+        FX[pl.ds(o + BY, BY), :] = E[pl.ds(o, BY), :] * vel_o[VX, pl.ds(o, BY), :]
+        return carry
+
+    lax.fori_loop(0, BX, xflux, 0, unroll=8)
+    for side in range(2):
+        xsend2[side] = FX[pl.ds(BY if side == 0 else ROWS, BY), :]
+
+    def xcopy2(side):
+        return remote(
+            xsend2.at[side], FX.at[pl.ds(ROWS + BY if side == 0 else 0, BY), :],
+            xs2.at[side], xr2.at[1 - side], xlow if side == 0 else xhigh,
+        )
+
+    when_each(xhas, lambda side: xcopy2(side).start())
+
+    when_each(yhas, lambda side: mcopy(1 - side, 2).wait_recv())
     for side in range(2):
         zcopy(1 - side, zsend2, zrecv2, zs2, zr2).wait_recv()
     Q[0:1, :] = zrecv2[1, 0:1, :]
@@ -355,8 +487,8 @@
         h = pltpu.roll(S[pl.ds(o, BY), :], BZ - 1, 1)
         d = FX[pl.ds(o + 2 * BY, BY), :] - FX[pl.ds(o, BY), :]
         d = d + (
-            jnp.where(rown == BY - 1, yrecv[1, FC, pl.ds(x, 1), :], pltpu.roll(fy, BY - 1, 0))
-            - jnp.where(rown == 0, yrecv[0, FC, pl.ds(x, 1), :], pltpu.roll(fy, 1, 0))
+            jnp.where(rown == BY - 1, yrecv[1, NF_, pl.ds(x, 1), :], pltpu.roll(fy, BY - 1, 0))
+            - jnp.where(rown == 0, yrecv[0, NF_, pl.ds(x, 1), :], pltpu.roll(fy, 1, 0))
         )
         d = d + (
             jnp.where(lane == BZ - 1, h, pltpu.roll(fz, BZ - 1, 1))
@@ -365,10 +497,9 @@
         src_o[pl.ds(o, BY), :] = 0.5 * d
         return carry
 
-    lax.fori_loop(0, BX, diverge, 0)
-
-    for k in range(1, 32):
-        c2(k).wait_recv()
+    lax.fori_loop(0, BX, diverge, 0, unroll=4)
+
+    all_of(red2, 31, s2, r2).wait_recv()
     total = red2[0]
     for i in range(1, 32):
         total = total + red2[i]
@@ -380,15 +511,26 @@
     aux_o[0:1, :] = jnp.broadcast_to(DT * step, (1, BZ))
     aux_o[1:2, :] = jnp.broadcast_to(force + step, (1, BZ))
 
-    when_each(yhas, lambda side: [ycopy(side, f).wait_send() for f in range(6)] and None)
+    for kind in range(2):
+        @pl.when(paired(kind))
+        def _():
+            for j in range(3):
+                ycopy(kind, j).wait_send()
+
+    @pl.when(middle)
+    def _():
+        both(lambda q: [mcopy(q, j).wait_send() for j in range(3)])
+
     when_each(xhas, lambda side: (xcopy(side).wait_send(), xcopy2(side).wait_send()) and None)
+    @pl.when(relay)
+    def _():
+        zforward().wait_send()
+
     for side in range(2):
         zcopy(side, zsend, zrecv, zs, zr).wait_send()
         zcopy(side, zsend2, zrecv2, zs2, zr2).wait_send()
-    for k in range(1, 16):
-        c1(k).wait_send()
-    for k in range(1, 32):
-        c2(k).wait_send()
+    all_of(red1, 15, s1, r1).wait_send()
+    all_of(red2, 31, s2, r2).wait_send()
 
 
 def finish(vel, src, slope, aux, vel_o, src_o, force_o, vz, out, sem):
@@ -438,15 +580,20 @@
             pltpu.VMEM((2, 8, ROWS), f32),
             pltpu.VMEM((2, 8, ROWS), f32),
             pltpu.VMEM((2, 6, BX, BZ), f32),
+            pltpu.VMEM((2, 4, BX, BZ), f32),
+            pltpu.VMEM((2, 4, BX, BZ), f32),
             pltpu.VMEM((2, 6, BX, BZ), f32),
+            pltpu.VMEM((BX, BZ), f32),
             pltpu.VMEM((2, BY, BZ), f32),
+            pltpu.VMEM((8, ROWS), f32),
             pltpu.VMEM((1, 1, BZ), f32),
             pltpu.VMEM((16, 1, BZ), f32),
             pltpu.VMEM((1, 1, BZ), f32),
             pltpu.VMEM((32, 1, BZ), f32),
             dma((6,)), dma((2,)), dma((2,)), dma((2,)), dma((2,)), dma((2,)), dma((2,)),
-            dma((2, 6)), dma((2, 6)), dma((2,)), dma((2,)),
-            dma((16,)), dma((16,)), dma((32,)), dma((32,)),
+            dma((2, 3)), dma((2, 3)), dma((2, 3)), dma((2, 3)), dma((2,)), dma((2,)),
+            dma, dma, dma, dma, pltpu.SemaphoreType.REGULAR((3, 2)), pltpu.SemaphoreType.REGULAR((4,)),
+            pltpu.SemaphoreType.REGULAR, dma, dma,
         ],
         compiler_params=pltpu.CompilerParams(collective_id=0, has_side_effects=True),
     )(

time: 52.5 us -> 45 us (0.86)
  Pallas kernels: 50.1 us -> 42.9 us
    pallas_call x1, Pallas kernels: 48.6 us -> 41.4 us  [local(): pl.pallas_call(kernel, out_shape=(pltpu.VMEM((3, ROWS, BZ), f32), pltpu.V...]
where the time goes in v3:
time: 45 us; the launch traced here: 44.9 us
  Pallas kernels  42.9 us (95%)
  between operations  1.93 us (4%)
    pallas_call x1, Pallas kernels, local(): pl.pallas_call(kernel, out_shape=(pltpu.VMEM((3, ROWS, BZ), f32), pltpu.V...  41.4 us
    pallas_call x1, Pallas kernels, local(): pl.pallas_call(finish, out_shape=(jax.ShapeDtypeStruct((3, ROWS, BZ), f32...  1.5 us

profile of v3, /device:TPU:1, one launch (start us, length us, event | category | flops | bytes accessed | tf_op | source)
XLA Modules:
  0.0 44.9 jit_solution(18358149826231214727)
XLA Ops:
  1.9 41.4 %shard_map.85 = (f32[3,512,128]{2,1,0:T(8,128)S(1)}, f32[512,128]{1,0:T(8,128)S(1)}, f32[512,128]{1,0:T(8,128)S(1)}, f32[8,128]{1,0:T(8,128)S(1)}) custom-call(f32[1]{0:T(128)S(6)} %copy.9.force_h, f32[1]{0:T(128)S(6)} %copy.10.target_h, f32[3,512,128]{2,1,0:T(8,128)} %bitcast.7, f32[512,128]{1,0:T(8,128)} %bitcast.9, f32[512,128]{1,0:T(8,128)} %bitcast.10, ...), custom_call_target="tpu_custom_call" | custom-call | tf_op jit(solution)/shard_map/pallas_call | solution.py:558
  43.4 1.5 %shard_map.86 = (f32[3,512,128]{2,1,0:T(8,128)}, f32[512,128]{1,0:T(8,128)}, f32[1,1]{1,0:T(1,128)}) custom-call(f32[3,512,128]{2,1,0:T(8,128)S(1)} %get-tuple-element.10.vel, f32[512,128]{1,0:T(8,128)S(1)} %get-tuple-element.11.src, f32[512,128]{1,0:T(8,128)S(1)} %get-tuple-element.12.slope, f32[8,128]{1,0:T(8,128)S(1)} %get-tuple-element.13.aux), custom_call_target="tpu_custom_call" | custom-call | tf_op jit(solution)/shard_map/pallas_call | solution.py:607

commit v4 on v3

--- a/solution.py
+++ b/solution.py
@@ -31,7 +31,7 @@
     V, E, PV, G, S, FX, Q, scal,
     xrecv, zsend, zrecv, zsend2, zrecv2, ysend, yrecv, msend, mrecv, yacc, xsend2, rbuf,
     row1, red1, row2, red2,
-    lsem, xs, xr, zs, zr, zs2, zr2, ys, yr, ms, mr, xs2, xr2, s1, r1, s2, r2, know, wave, cross, rsem, fsem,
+    lsem, xs, xr, zs, zr, zs2, zr2, ys, yr, ms, mr, xs2, xr2, s1, r1, s2, r2, know, wave, rsem, fsem,
 ):
     gz, gy, gx = lax.axis_index("gz"), lax.axis_index("gy"), lax.axis_index("gx")
     ngz, ngy, ngx = 16, 8, 4
@@ -61,12 +61,16 @@
     xlow, xhigh = at(gx=lax.rem(gx + ngx - 1, ngx)), at(gx=lax.rem(gx + 1, ngx))
 
     barrier = pltpu.get_barrier_semaphore()
-    below, above = [of_z(zabs + 16 - k) for k in (1, 2, 4)], [of_z(zabs + k) for k in (1, 2, 4)]
     yprev, ynext = of_z(zabs, -1), of_z(zabs, 1)
     other = at(gz=zlo * 2 + 1 - core)
     outer_far = (gz == 0) | (gz == ngz - 1)
     outer = at(gz=lax.rem(gz + ngz - 1 + 2 * core, ngz))
-    nearest = [below[0], above[0], other, xlow, xhigh, yprev, ynext]
+    across_z = lax.rem(zabs + 19 - 6 * core, 16)
+    across = at(gz=lax.rem(across_z, 8) * 2 + 1 - core, gy=y * 2 + across_z // 8)
+    nearest = [of_z(zabs + 16 + k) for k in (-4, 4, -3, 3, -2, 2, -1, 1)]
+    below, above = nearest[:2]
+    nearest += [of_z(zabs + 4, 1), of_z(zabs + 12, -1), across]
+    nearest += [xlow, xhigh, yprev, ynext, other]
     for d in nearest:
         pl.semaphore_signal(barrier, inc=1, device_id=d, device_id_type=MESH)
 
@@ -92,26 +96,6 @@
         V[f, pl.ds(0, BY), :] = zero
         V[f, pl.ds(ROWS + BY, BY), :] = zero
     Q[...] = jnp.zeros_like(Q)
-    def tell(step):
-        pl.semaphore_signal(know.at[step, 0], inc=1, device_id=above[step], device_id_type=MESH)
-        pl.semaphore_signal(know.at[step, 1], inc=1, device_id=below[step], device_id_type=MESH)
-
-    def heard(step, side):
-        pl.semaphore_wait(know.at[step, side], 1)
-
-    waves = [(xlow, xhigh), (yprev, ynext), (yprev, ynext), (other,)]
-
-    def plane_tell(i):
-        for d in waves[i]:
-            pl.semaphore_signal(wave.at[i], inc=1, device_id=d, device_id_type=MESH)
-
-    def plane_heard(i):
-        pl.semaphore_wait(wave.at[i], len(waves[i]))
-
-    pl.semaphore_wait(barrier, len(nearest) + jnp.where(outer_far, 0, 1))
-    tell(0)
-    plane_tell(0)
-
     for cp in loads:
         cp.wait()
     force, target = scal[0, 0], scal[1, 0]
@@ -127,10 +111,6 @@
         e = E[rows, :]
         ysend[side, FD] = e * DT * weight(v, [PV[k, rows, :] for k in range(3)], e)[1]
 
-    heard(0, 0)
-    heard(0, 1)
-    tell(1)
-
     def remote(src, dst, a, b, dev):
         return pltpu.make_async_remote_copy(
             src_ref=src, dst_ref=dst, send_sem=a, recv_sem=b, device_id=dev, device_id_type=MESH
@@ -151,7 +131,7 @@
 
     def mwait(q, j):
         part = pl.ds(*GROUPS[j])
-        remote(ysend.at[0, part], mrecv.at[q, part], ys.at[0, j], mr.at[q, j], above[2]).wait_recv()
+        remote(ysend.at[0, part], mrecv.at[q, part], ys.at[0, j], mr.at[q, j], above).wait_recv()
 
     def yhas(side):
         return has_ylo if side == 0 else has_yhi
@@ -192,9 +172,18 @@
             for g in groups:
                 ycopy(kind, g).start()
 
-    when_each(xhas, lambda side: xcopy(side).start())
-    plane_heard(0)
-    plane_tell(1)
+    def heard():
+        pl.semaphore_wait(know.at[0], 1)
+        pl.semaphore_wait(know.at[1], 1)
+
+    waves = [(xlow, xhigh), (yprev, ynext), (yprev, ynext), (other,)]
+
+    def plane_tell(i):
+        for d in waves[i]:
+            pl.semaphore_signal(wave.at[i], inc=1, device_id=d, device_id_type=MESH)
+
+    def plane_heard(i):
+        pl.semaphore_wait(wave.at[i], len(waves[i]))
 
     def columns(x, carry):
         o = pl.multiple_of(x * BY, BY)
@@ -207,13 +196,13 @@
 
     lax.fori_loop(0, BX, columns, 0, unroll=4)
 
-    def pack(dst):
+    def pack(dst, n):
         for i in range(4):
             t = S[pl.ds(BZ * i, BZ), :].T
-            dst[0, :, pl.ds(BZ * i, BZ)] = t[0:8]
-            dst[1, :, pl.ds(BZ * i, BZ)] = t[8:16]
-
-    pack(zsend)
+            dst[0, :, pl.ds(BZ * i, BZ)] = t[0:n]
+            dst[1, :, pl.ds(BZ * i, BZ)] = t[8:8 + n]
+
+    pack(zsend, 8)
     relay = zlo == 4 - core
 
     def zwrap():
@@ -226,32 +215,23 @@
             rbuf, zrecv.at[1 - core], fsem, zr.at[1 - core], at(gz=gz + 7 - 14 * core),
         )
 
+    pl.semaphore_wait(barrier, len(nearest) + jnp.where(outer_far, 0, 1))
+    @pl.when(outer_far)
+    def _():
+        zwrap().start()
+
     for side in range(2):
         @pl.when(jnp.logical_not(outer_far & (core == side)))
         def _():
             zcopy(side, zsend, zrecv, zs, zr).start()
 
-    heard(1, 1 - zhi)
     send_y(0, (0,))
-    heard(1, zhi)
-
-    tell(2)
-
-    @pl.when(outer_far)
-    def _():
-        zwrap().start()
-
-    @pl.when(zhi == 1)
-    def _():
-        pl.semaphore_signal(
-            cross, inc=1, device_id=of_z(zabs, -1), device_id_type=MESH
-        )
-        pl.semaphore_wait(cross, 1)
-
     send_y(1, (0,))
-
-    plane_heard(1)
-    plane_tell(2)
+    when_each(xhas, lambda side: xcopy(side).start())
+
+    pl.semaphore_signal(know.at[0], inc=1, device_id=above, device_id_type=MESH)
+    pl.semaphore_signal(know.at[1], inc=1, device_id=below, device_id_type=MESH)
+    plane_tell(0)
 
     def slab(x, carry):
         o = pl.multiple_of(x * BY, BY)
@@ -280,15 +260,21 @@
         return carry
 
     lax.fori_loop(0, BX, slab, 0, unroll=4)
-    send_y(0, (1,))
-    send_y(1, (1,))
-    plane_heard(2)
-    plane_tell(3)
+    plane_heard(0)
+    plane_tell(1)
+
+    @pl.when(outer_far)
+    def _():
+        send_y(0, (1,))
+        send_y(1, (1,))
 
     @pl.when(relay)
     def _():
         zwrap().wait_recv()
         zforward().start()
+
+    plane_heard(1)
+    plane_tell(2)
 
     def not_(has):
         return lambda side: jnp.logical_not(has(side))
@@ -362,6 +348,14 @@
     for side in range(2):
         rows = pl.ds(face(side), BX, stride=BY)
         ysend[side, FC] = E[rows, :] * vel_o[VY, rows, :]
+    plane_heard(2)
+    plane_tell(3)
+
+    @pl.when(jnp.logical_not(outer_far))
+    def _():
+        send_y(0, (1,))
+        send_y(1, (1,))
+
     send_y(0, (2,))
     send_y(1, (2,))
 
@@ -401,8 +395,7 @@
     def c2(k):
         return remote(row2.at[0], red2.at[plane], s2, r2, ppeers[k - 1])
 
-    heard(2, 0)
-    heard(2, 1)
+    heard()
     for k in range(1, 16):
         c1(k).start()
 
@@ -413,34 +406,16 @@
         couple(VY, FVY, NY_)
         couple(VX, FVX, NX_)
         both(lambda q: mcopy(q, 1).start())
+
+    @pl.when(middle)
+    def _():
         both(lambda q: mwait(q, 2))
         for q in range(2):
             msend[q, NF_] = mrecv[1 - q, FC] + mrecv[1 - q, FD] * msend[1 - q, NY_]
         both(lambda q: mcopy(q, 2).start())
 
-    def yback(j, terms):
-        when_each(yhas, lambda side: mcopy(1 - side, j).wait_recv())
-        for side in range(2):
-            rows = pl.ds(face(side), BX, stride=BY)
-            g = G[rows, :]
-            for k, n in terms:
-                vel_o[k, rows, :] = vel_o[k, rows, :] + g * yrecv[side, n]
-
-    yback(0, ((VZ, NZ_),))
-
-    def zflux(x, carry):
-        o = pl.multiple_of(x * BY, BY)
-        fz = E[pl.ds(o, BY), :] * vel_o[VZ, pl.ds(o, BY), :]
-        S[pl.ds(o, BY), :] = jnp.where(lane == 8, pltpu.roll(fz, 9, 1), fz)
-        return carry
-
-    lax.fori_loop(0, BX, zflux, 0, unroll=8)
-    pack(zsend2)
-    for side in range(2):
-        zcopy(side, zsend2, zrecv2, zs2, zr2).start()
-
     def all_of(red, n, a, b):
-        return remote(red.at[pl.ds(0, n)], red.at[pl.ds(0, n)], a, b, above[2])
+        return remote(red.at[pl.ds(0, n)], red.at[pl.ds(0, n)], a, b, above)
 
     all_of(red1, 15, s1, r1).wait_recv()
     part2 = red1[0]
@@ -451,6 +426,27 @@
     plane_heard(3)
     for k in range(1, 32):
         c2(k).start()
+
+    def yback(j, terms):
+        when_each(yhas, lambda side: mcopy(1 - side, j).wait_recv())
+        for side in range(2):
+            rows = pl.ds(face(side), BX, stride=BY)
+            g = G[rows, :]
+            for k, n in terms:
+                vel_o[k, rows, :] = vel_o[k, rows, :] + g * yrecv[side, n]
+
+    yback(0, ((VZ, NZ_),))
+
+    def zflux(x, carry):
+        o = pl.multiple_of(x * BY, BY)
+        fz = E[pl.ds(o, BY), :] * vel_o[VZ, pl.ds(o, BY), :]
+        S[pl.ds(o, BY), :] = jnp.where(lane == 8, pltpu.roll(fz, 9, 1), fz)
+        return carry
+
+    lax.fori_loop(0, BX, zflux, 0, unroll=8)
+    pack(zsend2, 1)
+    for side in range(2):
+        zcopy(side, zsend2, zrecv2, zs2, zr2).start()
 
     yback(1, ((VX, NX_), (VY, NY_)))
 
@@ -577,8 +573,8 @@
             pltpu.VMEM((2, 4, BY, BZ), f32),
             pltpu.VMEM((2, 8, ROWS), f32),
             pltpu.VMEM((2, 8, ROWS), f32),
-            pltpu.VMEM((2, 8, ROWS), f32),
-            pltpu.VMEM((2, 8, ROWS), f32),
+            pltpu.VMEM((2, 1, ROWS), f32),
+            pltpu.VMEM((2, 1, ROWS), f32),
             pltpu.VMEM((2, 6, BX, BZ), f32),
             pltpu.VMEM((2, 4, BX, BZ), f32),
             pltpu.VMEM((2, 4, BX, BZ), f32),
@@ -592,8 +588,7 @@
             pltpu.VMEM((32, 1, BZ), f32),
             dma((6,)), dma((2,)), dma((2,)), dma((2,)), dma((2,)), dma((2,)), dma((2,)),
             dma((2, 3)), dma((2, 3)), dma((2, 3)), dma((2, 3)), dma((2,)), dma((2,)),
-            dma, dma, dma, dma, pltpu.SemaphoreType.REGULAR((3, 2)), pltpu.SemaphoreType.REGULAR((4,)),
-            pltpu.SemaphoreType.REGULAR, dma, dma,
+            dma, dma, dma, dma, pltpu.SemaphoreType.REGULAR((2,)), pltpu.SemaphoreType.REGULAR((4,)), dma, dma,
         ],
         compiler_params=pltpu.CompilerParams(collective_id=0, has_side_effects=True),
     )(

time: 45 us -> 42.7 us (0.949)
  Pallas kernels: 42.9 us -> 40.6 us
    pallas_call x1, Pallas kernels: 41.4 us -> 39.1 us  [local(): pl.pallas_call(kernel, out_shape=(pltpu.VMEM((3, ROWS, BZ), f32), pltpu.V...]
where the time goes in v4:
time: 42.7 us; the launch traced here: 42.5 us
  Pallas kernels  40.6 us (95%)
  between operations  1.93 us (5%)
    pallas_call x1, Pallas kernels, local(): pl.pallas_call(kernel, out_shape=(pltpu.VMEM((3, ROWS, BZ), f32), pltpu.V...  39.1 us
    pallas_call x1, Pallas kernels, local(): pl.pallas_call(finish, out_shape=(jax.ShapeDtypeStruct((3, ROWS, BZ), f32...  1.5 us

profile of v4, /device:TPU:1, one launch (start us, length us, event | category | flops | bytes accessed | tf_op | source)
XLA Modules:
  0.0 42.5 jit_solution(6807075824568073890)
XLA Ops:
  1.9 39.1 %shard_map.85 = (f32[3,512,128]{2,1,0:T(8,128)S(1)}, f32[512,128]{1,0:T(8,128)S(1)}, f32[512,128]{1,0:T(8,128)S(1)}, f32[8,128]{1,0:T(8,128)S(1)}) custom-call(f32[1]{0:T(128)S(6)} %copy.9.force_h, f32[1]{0:T(128)S(6)} %copy.10.target_h, f32[3,512,128]{2,1,0:T(8,128)} %bitcast.7, f32[512,128]{1,0:T(8,128)} %bitcast.9, f32[512,128]{1,0:T(8,128)} %bitcast.10, ...), custom_call_target="tpu_custom_call" | custom-call | tf_op jit(solution)/shard_map/pallas_call | solution.py:554
  41.0 1.5 %shard_map.86 = (f32[3,512,128]{2,1,0:T(8,128)}, f32[512,128]{1,0:T(8,128)}, f32[1,1]{1,0:T(1,128)}) custom-call(f32[3,512,128]{2,1,0:T(8,128)S(1)} %get-tuple-element.10.vel, f32[512,128]{1,0:T(8,128)S(1)} %get-tuple-element.11.src, f32[512,128]{1,0:T(8,128)S(1)} %get-tuple-element.12.slope, f32[8,128]{1,0:T(8,128)S(1)} %get-tuple-element.13.aux), custom_call_target="tpu_custom_call" | custom-call | tf_op jit(solution)/shard_map/pallas_call | solution.py:602

commit v5 on v4

--- a/solution.py
+++ b/solution.py
@@ -27,8 +27,8 @@
 
 def kernel(
     force_h, target_h, vel_h, pres_h, eps_h, pv_h,
-    vel_o, src_o, SL, aux_o,
-    V, E, PV, G, S, FX, Q, scal,
+    vel_o, src_o, SL, aux_o, S,
+    V, E, PV, G, FX, Q, scal,
     xrecv, zsend, zrecv, zsend2, zrecv2, ysend, yrecv, msend, mrecv, yacc, xsend2, rbuf,
     row1, red1, row2, red2,
     lsem, xs, xr, zs, zr, zs2, zr2, ys, yr, ms, mr, xs2, xr2, s1, r1, s2, r2, know, wave, rsem, fsem,
@@ -199,10 +199,11 @@
     def pack(dst, n):
         for i in range(4):
             t = S[pl.ds(BZ * i, BZ), :].T
-            dst[0, :, pl.ds(BZ * i, BZ)] = t[0:n]
-            dst[1, :, pl.ds(BZ * i, BZ)] = t[8:8 + n]
-
-    pack(zsend, 8)
+            for k in range(n):
+                dst[0, k, :, pl.ds(BZ * i, BZ)] = t[k:k + 1]
+                dst[1, k, :, pl.ds(BZ * i, BZ)] = t[8 + k:9 + k]
+
+    pack(zsend, 5)
     relay = zlo == 4 - core
 
     def zwrap():
@@ -310,17 +311,17 @@
         zcopy(1 - side, zsend, zrecv, zs, zr).wait_recv()
     for i in range(4):
         ln = pl.ds(BZ * i, BZ)
-        vlo, vhi = zsend[0, 2:3, ln], zsend[1, 2:3, ln]
+        vlo, vhi = zsend[0, 2, :, ln], zsend[1, 2, :, ln]
         clo, chi = NU + 0.5 * vlo, NU - 0.5 * vhi
         for k in range(3):
-            nlo, nhi = clo * zrecv[0, k:k + 1, ln], chi * zrecv[1, k:k + 1, ln]
+            nlo, nhi = clo * zrecv[0, k, :, ln], chi * zrecv[1, k, :, ln]
             if k == 2:
-                nlo = nlo + 0.5 * zrecv[0, 3:4, ln]
-                nhi = nhi - 0.5 * zrecv[1, 3:4, ln]
+                nlo = nlo + 0.5 * zrecv[0, 3, :, ln]
+                nhi = nhi - 0.5 * zrecv[1, 3, :, ln]
             Q[2 * k:2 * k + 1, ln] = nhi
             Q[2 * k + 1:2 * k + 2, ln] = nlo
-        Q[6:7, ln] = zrecv[1, 4:5, ln]
-        Q[7:8, ln] = zrecv[0, 4:5, ln]
+        Q[6:7, ln] = zrecv[1, 4, :, ln]
+        Q[7:8, ln] = zrecv[0, 4, :, ln]
 
     def unpack():
         for i in range(4):
@@ -414,6 +415,30 @@
             msend[q, NF_] = mrecv[1 - q, FC] + mrecv[1 - q, FD] * msend[1 - q, NY_]
         both(lambda q: mcopy(q, 2).start())
 
+    def yback(j, terms):
+        when_each(yhas, lambda side: mcopy(1 - side, j).wait_recv())
+        for side in range(2):
+            rows = pl.ds(face(side), BX, stride=BY)
+            g = G[rows, :]
+            for k, n in terms:
+                vel_o[k, rows, :] = vel_o[k, rows, :] + g * yrecv[side, n]
+
+    def zstep():
+        yback(0, ((VZ, NZ_),))
+
+        def zflux(x, carry):
+            o = pl.multiple_of(x * BY, BY)
+            fz = E[pl.ds(o, BY), :] * vel_o[VZ, pl.ds(o, BY), :]
+            S[pl.ds(o, BY), :] = jnp.where(lane == 8, pltpu.roll(fz, 9, 1), fz)
+            return carry
+
+        lax.fori_loop(0, BX, zflux, 0, unroll=8)
+        pack(zsend2, 1)
+        for side in range(2):
+            zcopy(side, zsend2, zrecv2, zs2, zr2).start()
+
+    pl.when(gz == ngz - 1)(zstep)
+
     def all_of(red, n, a, b):
         return remote(red.at[pl.ds(0, n)], red.at[pl.ds(0, n)], a, b, above)
 
@@ -427,26 +452,7 @@
     for k in range(1, 32):
         c2(k).start()
 
-    def yback(j, terms):
-        when_each(yhas, lambda side: mcopy(1 - side, j).wait_recv())
-        for side in range(2):
-            rows = pl.ds(face(side), BX, stride=BY)
-            g = G[rows, :]
-            for k, n in terms:
-                vel_o[k, rows, :] = vel_o[k, rows, :] + g * yrecv[side, n]
-
-    yback(0, ((VZ, NZ_),))
-
-    def zflux(x, carry):
-        o = pl.multiple_of(x * BY, BY)
-        fz = E[pl.ds(o, BY), :] * vel_o[VZ, pl.ds(o, BY), :]
-        S[pl.ds(o, BY), :] = jnp.where(lane == 8, pltpu.roll(fz, 9, 1), fz)
-        return carry
-
-    lax.fori_loop(0, BX, zflux, 0, unroll=8)
-    pack(zsend2, 1)
-    for side in range(2):
-        zcopy(side, zsend2, zrecv2, zs2, zr2).start()
+    pl.when(gz < ngz - 1)(zstep)
 
     yback(1, ((VX, NX_), (VY, NY_)))
 
@@ -468,11 +474,6 @@
     when_each(xhas, lambda side: xcopy2(side).start())
 
     when_each(yhas, lambda side: mcopy(1 - side, 2).wait_recv())
-    for side in range(2):
-        zcopy(1 - side, zsend2, zrecv2, zs2, zr2).wait_recv()
-    Q[0:1, :] = zrecv2[1, 0:1, :]
-    Q[1:2, :] = zrecv2[0, 0:1, :]
-    unpack()
     when_each(xhas, lambda side: xcopy2(1 - side).wait_recv())
 
     def diverge(x, carry):
@@ -480,21 +481,25 @@
         e = E[pl.ds(o, BY), :]
         fy = e * vel_o[VY, pl.ds(o, BY), :]
         fz = e * vel_o[VZ, pl.ds(o, BY), :]
-        h = pltpu.roll(S[pl.ds(o, BY), :], BZ - 1, 1)
         d = FX[pl.ds(o + 2 * BY, BY), :] - FX[pl.ds(o, BY), :]
         d = d + (
             jnp.where(rown == BY - 1, yrecv[1, NF_, pl.ds(x, 1), :], pltpu.roll(fy, BY - 1, 0))
             - jnp.where(rown == 0, yrecv[0, NF_, pl.ds(x, 1), :], pltpu.roll(fy, 1, 0))
         )
         d = d + (
-            jnp.where(lane == BZ - 1, h, pltpu.roll(fz, BZ - 1, 1))
-            - jnp.where(lane == 0, h, pltpu.roll(fz, 1, 1))
+            jnp.where(lane == BZ - 1, 0.0, pltpu.roll(fz, BZ - 1, 1))
+            - jnp.where(lane == 0, 0.0, pltpu.roll(fz, 1, 1))
         )
         src_o[pl.ds(o, BY), :] = 0.5 * d
         return carry
 
     lax.fori_loop(0, BX, diverge, 0, unroll=4)
 
+    for side in range(2):
+        zcopy(1 - side, zsend2, zrecv2, zs2, zr2).wait_recv()
+    Q[0:1, :] = zrecv2[1, 0]
+    Q[1:2, :] = zrecv2[0, 0]
+    unpack()
     all_of(red2, 31, s2, r2).wait_recv()
     total = red2[0]
     for i in range(1, 32):
@@ -529,7 +534,7 @@
     all_of(red2, 31, s2, r2).wait_send()
 
 
-def finish(vel, src, slope, aux, vel_o, src_o, force_o, vz, out, sem):
+def finish(vel, src, slope, aux, halo, vel_o, src_o, force_o, vz, out, sem):
     pairs = [
         pltpu.make_async_copy(vel.at[pl.ds(0, 2)], vel_o.at[pl.ds(0, 2)], sem.at[0]),
         pltpu.make_async_copy(vz, vel_o.at[VZ], sem.at[1]),
@@ -540,7 +545,9 @@
     add = aux[0:1, :]
     vz[...] = vel[VZ] + add
     pairs[1].start()
-    out[...] = src[...] + add * slope[...]
+    lane = lax.broadcasted_iota(jnp.int32, (ROWS, BZ), 1)
+    sign = jnp.where(lane == 0, -0.5, jnp.where(lane == BZ - 1, 0.5, 0.0))
+    out[...] = src[...] + add * slope[...] + sign * pltpu.roll(halo[...], BZ - 1, 1)
     pairs[2].start()
     for cp in pairs:
         cp.wait()
@@ -558,30 +565,30 @@
             pltpu.VMEM((ROWS, BZ), f32),
             pltpu.VMEM((ROWS, BZ), f32),
             pltpu.VMEM((8, BZ), f32),
+            pltpu.VMEM((ROWS, BZ), f32),
         ),
         in_specs=[pl.BlockSpec(memory_space=pltpu.HBM)] * 6,
-        out_specs=(vmem,) * 4,
+        out_specs=(vmem,) * 5,
         scratch_shapes=[
             pltpu.VMEM((4, PAD, BZ), f32),
             pltpu.VMEM((ROWS, BZ), f32),
             pltpu.VMEM((3, ROWS, BZ), f32),
             pltpu.VMEM((ROWS, BZ), f32),
-            pltpu.VMEM((ROWS, BZ), f32),
             pltpu.VMEM((PAD, BZ), f32),
             pltpu.VMEM((BZ, ROWS), f32),
             pltpu.SMEM((2, 1), f32),
             pltpu.VMEM((2, 4, BY, BZ), f32),
-            pltpu.VMEM((2, 8, ROWS), f32),
-            pltpu.VMEM((2, 8, ROWS), f32),
-            pltpu.VMEM((2, 1, ROWS), f32),
-            pltpu.VMEM((2, 1, ROWS), f32),
+            pltpu.VMEM((2, 5, 1, ROWS), f32),
+            pltpu.VMEM((2, 5, 1, ROWS), f32),
+            pltpu.VMEM((2, 1, 1, ROWS), f32),
+            pltpu.VMEM((2, 1, 1, ROWS), f32),
             pltpu.VMEM((2, 6, BX, BZ), f32),
             pltpu.VMEM((2, 4, BX, BZ), f32),
             pltpu.VMEM((2, 4, BX, BZ), f32),
             pltpu.VMEM((2, 6, BX, BZ), f32),
             pltpu.VMEM((BX, BZ), f32),
             pltpu.VMEM((2, BY, BZ), f32),
-            pltpu.VMEM((8, ROWS), f32),
+            pltpu.VMEM((5, 1, ROWS), f32),
             pltpu.VMEM((1, 1, BZ), f32),
             pltpu.VMEM((16, 1, BZ), f32),
             pltpu.VMEM((1, 1, BZ), f32),
@@ -606,7 +613,7 @@
             jax.ShapeDtypeStruct((ROWS, BZ), f32),
             jax.ShapeDtypeStruct((1, 1), f32),
         ),
-        in_specs=[vmem] * 4,
+        in_specs=[vmem] * 5,
         out_specs=(hbm, hbm, vmem),
         scratch_shapes=[pltpu.VMEM((ROWS, BZ), f32), pltpu.VMEM((ROWS, BZ), f32), dma((3,))],
         compiler_params=pltpu.CompilerParams(vmem_limit_bytes=8 * 1024 * 1024),

time: 42.7 us -> 42.6 us (level)
  no operation moved by 1% of the time
where the time goes in v5:
time: 42.6 us; the launch traced here: 42.4 us
  Pallas kernels  40.5 us (95%)
  between operations  1.93 us (5%)
    pallas_call x1, Pallas kernels, local(): pl.pallas_call(kernel, out_shape=(pltpu.VMEM((3, ROWS, BZ), f32), pltpu.V...  38.9 us
    pallas_call x1, Pallas kernels, local(): pl.pallas_call(finish, out_shape=(jax.ShapeDtypeStruct((3, ROWS, BZ), f32...  1.53 us

profile of v5, /device:TPU:1, one launch (start us, length us, event | category | flops | bytes accessed | tf_op | source)
XLA Modules:
  0.0 42.4 jit_solution(10666084973896278251)
XLA Ops:
  1.9 38.9 %shard_map.85 = (f32[3,512,128]{2,1,0:T(8,128)S(1)}, f32[512,128]{1,0:T(8,128)S(1)}, f32[512,128]{1,0:T(8,128)S(1)}, f32[8,128]{1,0:T(8,128)S(1)}, f32[512,128]{1,0:T(8,128)S(1)}) custom-call(f32[1]{0:T(128)S(6)} %copy.9.force_h, f32[1]{0:T(128)S(6)} %copy.10.target_h, f32[3,512,128]{2,1,0:T(8,128)} %bitcast.7, f32[512,128]{1,0:T(8,128)} %bitcast.9, ...), custom_call_target="tpu_custom_call" | custom-call | tf_op jit(solution)/shard_map/pallas_call | solution.py:561
  40.9 1.5 %shard_map.86 = (f32[3,512,128]{2,1,0:T(8,128)}, f32[512,128]{1,0:T(8,128)}, f32[1,1]{1,0:T(1,128)}) custom-call(f32[3,512,128]{2,1,0:T(8,128)S(1)} %get-tuple-element.11.vel, f32[512,128]{1,0:T(8,128)S(1)} %get-tuple-element.12.src, f32[512,128]{1,0:T(8,128)S(1)} %get-tuple-element.13.slope, f32[8,128]{1,0:T(8,128)S(1)} %get-tuple-element.14.aux, ...), custom_call_target="tpu_custom_call" | custom-call | tf_op jit(solution)/shard_map/pallas_call | solution.py:609

commit v6 on v5

--- a/solution.py
+++ b/solution.py
@@ -194,7 +194,7 @@
         S[pl.ds(o, BY), :] = s
         return carry
 
-    lax.fori_loop(0, BX, columns, 0, unroll=4)
+    lax.fori_loop(0, BX, columns, 0, unroll=2)
 
     def pack(dst, n):
         for i in range(4):
@@ -432,7 +432,7 @@
             S[pl.ds(o, BY), :] = jnp.where(lane == 8, pltpu.roll(fz, 9, 1), fz)
             return carry
 
-        lax.fori_loop(0, BX, zflux, 0, unroll=8)
+        lax.fori_loop(0, BX, zflux, 0, unroll=4)
         pack(zsend2, 1)
         for side in range(2):
             zcopy(side, zsend2, zrecv2, zs2, zr2).start()
@@ -461,7 +461,7 @@
         FX[pl.ds(o + BY, BY), :] = E[pl.ds(o, BY), :] * vel_o[VX, pl.ds(o, BY), :]
         return carry
 
-    lax.fori_loop(0, BX, xflux, 0, unroll=8)
+    lax.fori_loop(0, BX, xflux, 0, unroll=4)
     for side in range(2):
         xsend2[side] = FX[pl.ds(BY if side == 0 else ROWS, BY), :]
 

time: 42.6 us -> 42.1 us (0.988)
  Pallas kernels: 40.5 us -> 40 us
    pallas_call x1, Pallas kernels: 38.9 us -> 38.4 us  [local(): pl.pallas_call(kernel, out_shape=(pltpu.VMEM((3, ROWS, BZ), f32), pltpu.V...]
where the time goes in v6:
time: 42.1 us; the launch traced here: 41.9 us
  Pallas kernels  40 us (95%)
  between operations  1.93 us (5%)
    pallas_call x1, Pallas kernels, local(): pl.pallas_call(kernel, out_shape=(pltpu.VMEM((3, ROWS, BZ), f32), pltpu.V...  38.4 us
    pallas_call x1, Pallas kernels, local(): pl.pallas_call(finish, out_shape=(jax.ShapeDtypeStruct((3, ROWS, BZ), f32...  1.53 us

profile of v6, /device:TPU:1, one launch (start us, length us, event | category | flops | bytes accessed | tf_op | source)
XLA Modules:
  0.0 41.9 jit_solution(16238702035882080683)
XLA Ops:
  1.9 38.4 %shard_map.85 = (f32[3,512,128]{2,1,0:T(8,128)S(1)}, f32[512,128]{1,0:T(8,128)S(1)}, f32[512,128]{1,0:T(8,128)S(1)}, f32[8,128]{1,0:T(8,128)S(1)}, f32[512,128]{1,0:T(8,128)S(1)}) custom-call(f32[1]{0:T(128)S(6)} %copy.9.force_h, f32[1]{0:T(128)S(6)} %copy.10.target_h, f32[3,512,128]{2,1,0:T(8,128)} %bitcast.7, f32[512,128]{1,0:T(8,128)} %bitcast.9, ...), custom_call_target="tpu_custom_call" | custom-call | tf_op jit(solution)/shard_map/pallas_call | solution.py:561
  40.4 1.5 %shard_map.86 = (f32[3,512,128]{2,1,0:T(8,128)}, f32[512,128]{1,0:T(8,128)}, f32[1,1]{1,0:T(1,128)}) custom-call(f32[3,512,128]{2,1,0:T(8,128)S(1)} %get-tuple-element.11.vel, f32[512,128]{1,0:T(8,128)S(1)} %get-tuple-element.12.src, f32[512,128]{1,0:T(8,128)S(1)} %get-tuple-element.13.slope, f32[8,128]{1,0:T(8,128)S(1)} %get-tuple-element.14.aux, ...), custom_call_target="tpu_custom_call" | custom-call | tf_op jit(solution)/shard_map/pallas_call | solution.py:609
